TPU v7x, 32 devices: a whole 2x2x4 slice. The times are simulated.
32 devices in a mesh: expert: 8 (over y, x, core), tensor: 4 (over z).
Axes of the slice: x: 2, y: 2, z: 4, core: 2. Of those that a mesh axis runs over, the one named last changes fastest.
Arguments:
- hidden_in: bfloat16 [2048, 2048], P('expert'), may hold values from -6 to 6
- segment_ids: int32 [8, 256], P('expert'), may hold values from 0 to 1, never falling along the last dimension, each value on 1 to 192 neighbouring positions
- expert_ids: int32 [2048, 6], P('expert'), may hold values from 0 to 15, all different within a row; in each aligned block of 256 rows (0 to 255, 256 to 511, ...) at most 192 rows name the same one
- query_weight: bfloat16 [2048, 3072], P('expert', 'tensor')
- latent_weight: bfloat16 [2048, 576], P('expert')
- expand_weight: bfloat16 [512, 4096], P('expert', 'tensor'), may hold values from -0.25 to 0.25
- output_weight: bfloat16 [2048, 2048], P('tensor', 'expert'), may hold values from -1 to 1
- prenorm: bfloat16 [2048], P('expert'), may hold values from 0.25 to 1.75
- latentnorm: bfloat16 [512], P('expert'), may hold values from 0.25 to 1.75
- postnorm: bfloat16 [2048], P('expert'), may hold values from 0.25 to 1.75
- router_weight: bfloat16 [2048, 16], P('expert'), may hold values from -0.125 to 0.125
- shared_gate: bfloat16 [2048, 2816], P('expert', 'tensor'), may hold values from -0.125 to 0.125
- shared_up: bfloat16 [2048, 2816], P('expert', 'tensor'), may hold values from -0.125 to 0.125
- shared_down: bfloat16 [2816, 2048], P('tensor', 'expert'), may hold values from -0.109375 to 0.109375
- expert_gate: bfloat16 [16, 2048, 1408], P('expert', None, 'tensor'), may hold values from -0.125 to 0.125
- expert_up: bfloat16 [16, 2048, 1408], P('expert', None, 'tensor'), may hold values from -0.125 to 0.125
- expert_down: bfloat16 [16, 1408, 2048], P('expert', 'tensor'), may hold values from -0.15625 to 0.15625
- cotangent: bfloat16 [2048, 2048], P('expert'), may hold values from -6 to 6
Outputs:
- block_output: bfloat16 [2048, 2048], P('expert')
- input_gradient: bfloat16 [2048, 2048], P('expert')
- query_gradient: float32 [2048, 3072], P('expert', 'tensor')
- latent_gradient: float32 [2048, 576], P('expert')
- expand_gradient: float32 [512, 4096], P('expert', 'tensor')
- output_gradient: float32 [2048, 2048], P('tensor', 'expert')
- prenorm_gradient: float32 [2048], P('expert')
- latentnorm_gradient: float32 [512], P('expert')
- postnorm_gradient: float32 [2048], P('expert')
- router_gradient: float32 [2048, 16], P('expert')
- shared_gate_gradient: float32 [2048, 2816], P('expert', 'tensor')
- shared_up_gradient: float32 [2048, 2816], P('expert', 'tensor')
- shared_down_gradient: float32 [2816, 2048], P('tensor', 'expert')
- expert_gate_gradient: float32 [16, 2048, 1408], P('expert', None, 'tensor')
- expert_up_gradient: float32 [16, 2048, 1408], P('expert', None, 'tensor')
- expert_down_gradient: float32 [16, 1408, 2048], P('expert', 'tensor')
Inputs may be any that keep to these rules, and one draw needn't show every extreme that they name: `segment_ids`: each sequence holds two documents, numbered 0 then 1: one of 64 to 192 positions and one of the rest, in either order. `expert_ids`: within the 256 rows of one sequence at most 192 pairs name any one expert, a bound that some block reaches.
All inputs are finite; a program needn't handle non-finite values.
Results may differ from a plain program's by a relative error of at most 0.025.
Values may be sent and summed in bfloat16 or wider, within the bound.
A program may use at most 320 MiB of HBM per device.

v0:
```python
import math

import jax
import jax.numpy as jnp
from jax import lax
from jax.sharding import PartitionSpec as P

D = 2048
HEAD_DIM = 128
ROPE_DIM = 64
KV_RANK = 512
TOP = 6


EPSILON = 1e-06
ROUTE_SCALE = 2.446
ROPE_BASE = 50000.0
MASKED = -1e30


def matmul(left, right):
    return jnp.dot(left, right, preferred_element_type=jnp.float32)


def matmul_nt(left, right):
    return lax.dot_general(
        left, right, (((1,), (1,)), ((), ())), preferred_element_type=jnp.float32
    )


def matmul_tn(left, right):
    return lax.dot_general(
        left, right, (((0,), (0,)), ((), ())), preferred_element_type=jnp.float32
    )


def rotary_tables(length):
    position = jnp.arange(length).astype(jnp.float32)
    exponent = jnp.arange(ROPE_DIM // 2).astype(jnp.float32) * (2.0 / ROPE_DIM)
    angles = position[:, None] * jnp.exp(-math.log(ROPE_BASE) * exponent)[None, :]
    return (jnp.cos(angles), jnp.sin(angles))


def rotate(values, cosine, sine):
    half = values.shape[-1] // 2
    first = values[..., :half]
    second = values[..., half:]
    return jnp.concatenate(
        [first * cosine - second * sine, second * cosine + first * sine], axis=-1
    )


def sigmoid(values):
    return 1.0 / (1.0 + jnp.exp(-values))


def slot_numbers(choices, experts):
    flat_choice = choices.reshape(-1)
    onehot = (flat_choice[:, None] == jnp.arange(experts, dtype=jnp.int32)[None, :]).astype(
        jnp.int32
    )
    earlier = jnp.cumsum(onehot, axis=0) - onehot
    return jnp.sum(earlier * onehot, axis=1).reshape(choices.shape)


def norm_backward(grad_normed, values, inverse, gain):
    gain_grad = jnp.sum(grad_normed * values * inverse, axis=0)
    scaled = grad_normed * gain
    inner = jnp.mean(scaled * values, axis=1, keepdims=True)
    return (inverse * scaled - values * inverse * inverse * inverse * inner, gain_grad)


def swiglu_backward(grad_hidden, gate_pre, up_pre):
    logistic = sigmoid(gate_pre)
    grad_up = (grad_hidden * gate_pre * logistic).astype(jnp.bfloat16)
    grad_gate = (grad_hidden * up_pre * logistic * (1.0 + gate_pre * (1.0 - logistic))).astype(
        jnp.bfloat16
    )
    return (grad_gate, grad_up)


def shards(
    hidden_in,
    segment_ids,
    expert_ids,
    query_weight,
    latent_weight,
    expand_weight,
    output_weight,
    prenorm,
    latentnorm,
    postnorm,
    router_weight,
    shared_gate,
    shared_up,
    shared_down,
    expert_gate,
    expert_up,
    expert_down,
    cotangent,
):
    groups = lax.axis_size("expert")
    ranks = lax.axis_size("tensor")
    local_experts = expert_gate.shape[0]
    experts = local_experts * groups
    length = hidden_in.shape[0]
    capacity = ranks * max(2, 2 * length * TOP // (experts * ranks))
    (
        query_full,
        latent_full,
        expand_full,
        output_full,
        pre_low,
        latent_low,
        post_low,
        router_full,
        common_gate,
        common_up,
        common_down,
    ) = (
        lax.all_gather(query_weight, "expert", axis=0, tiled=True),
        lax.all_gather(latent_weight, "expert", axis=0, tiled=True),
        lax.all_gather(expand_weight, "expert", axis=0, tiled=True),
        lax.all_gather(output_weight, "expert", axis=1, tiled=True),
        lax.all_gather(prenorm, "expert", axis=0, tiled=True),
        lax.all_gather(latentnorm, "expert", axis=0, tiled=True),
        lax.all_gather(postnorm, "expert", axis=0, tiled=True),
        lax.all_gather(router_weight, "expert", axis=0, tiled=True),
        lax.all_gather(shared_gate, "expert", axis=0, tiled=True),
        lax.all_gather(shared_up, "expert", axis=0, tiled=True),
        lax.all_gather(shared_down, "expert", axis=1, tiled=True),
    )
    pre_gain = pre_low.astype(jnp.float32)
    latent_gain = latent_low.astype(jnp.float32)
    post_gain = post_low.astype(jnp.float32)
    heads = query_full.shape[1] // (HEAD_DIM + ROPE_DIM)
    hidden = hidden_in.astype(jnp.float32)
    cosine, sine = rotary_tables(length)
    inverse_pre = lax.rsqrt(jnp.mean(hidden * hidden, axis=1, keepdims=True) + EPSILON)
    normed = (hidden * inverse_pre * pre_gain).astype(jnp.bfloat16)
    query_raw = matmul(normed, query_full).reshape(length, heads, HEAD_DIM + ROPE_DIM)
    query_nope = query_raw[:, :, :HEAD_DIM].astype(jnp.bfloat16)
    query_rope = rotate(query_raw[:, :, HEAD_DIM:], cosine[:, None, :], sine[:, None, :]).astype(
        jnp.bfloat16
    )
    latent_all = matmul(normed, latent_full)
    latent_raw = latent_all[:, :KV_RANK]
    inverse_latent = lax.rsqrt(jnp.mean(latent_raw * latent_raw, axis=1, keepdims=True) + EPSILON)
    compressed = (latent_raw * inverse_latent * latent_gain).astype(jnp.bfloat16)
    key_rope = rotate(latent_all[:, KV_RANK:], cosine, sine).astype(jnp.bfloat16)
    expanded = (
        matmul(compressed, expand_full).astype(jnp.bfloat16).reshape(length, heads, 2 * HEAD_DIM)
    )
    key_nope = expanded[:, :, :HEAD_DIM]
    values = expanded[:, :, HEAD_DIM:]
    scale = 1.0 / math.sqrt(HEAD_DIM + ROPE_DIM)
    position = jnp.arange(length)
    segments = segment_ids[0]
    allowed = ((position[None, :] <= position[:, None]) & (segments[:, None] == segments[None, :]))[
        None
    ]

    def score_block():
        raw = jnp.einsum("qhd,khd->hqk", query_nope, key_nope, preferred_element_type=jnp.float32)
        raw = raw + jnp.einsum(
            "qhr,kr->hqk", query_rope, key_rope, preferred_element_type=jnp.float32
        )
        return jnp.where(allowed, raw * scale, MASKED)

    scores = score_block()
    maxima = jnp.max(scores, axis=2, keepdims=True)
    weights = jnp.exp(scores - maxima)
    totals = jnp.sum(weights, axis=2, keepdims=True)
    probabilities = weights / totals
    log_total = maxima + jnp.log(totals)
    attended = (
        jnp.einsum(
            "hqk,khd->qhd",
            probabilities.astype(jnp.bfloat16),
            values,
            preferred_element_type=jnp.float32,
        )
        .astype(jnp.bfloat16)
        .reshape(length, heads * HEAD_DIM)
    )
    attention = lax.psum(matmul(attended, output_full), "tensor")
    middle = hidden + attention
    inverse_post = lax.rsqrt(jnp.mean(middle * middle, axis=1, keepdims=True) + EPSILON)
    normed_mid = (middle * inverse_post * post_gain).astype(jnp.bfloat16)
    affinity = sigmoid(matmul(normed_mid, router_full))
    onehot = (expert_ids[:, :, None] == jnp.arange(experts, dtype=jnp.int32)[None, None, :]).astype(
        jnp.float32
    )
    selected = jnp.sum(onehot * affinity[:, None, :], axis=2)
    selected_total = jnp.sum(selected, axis=1, keepdims=True)
    mixing = ROUTE_SCALE * selected / selected_total
    gate_pre = matmul(normed_mid, common_gate)
    up_pre = matmul(normed_mid, common_up)
    shared_hidden = (gate_pre * sigmoid(gate_pre) * up_pre).astype(jnp.bfloat16)
    shared_part = matmul(shared_hidden, common_down)
    slots = slot_numbers(expert_ids, experts)
    flat_rows = (expert_ids * capacity + slots).reshape(-1)
    outgoing = (
        jnp.zeros((experts * capacity, D), jnp.bfloat16)
        .at[flat_rows]
        .set(jnp.repeat(normed_mid, TOP, axis=0))
        .reshape(groups, local_experts, capacity, D)
    )
    received = lax.all_to_all(outgoing, "expert", split_axis=0, concat_axis=0, tiled=True)
    gate_routed = jnp.einsum(
        "secd,edf->secf", received, expert_gate, preferred_element_type=jnp.float32
    )
    up_routed = jnp.einsum(
        "secd,edf->secf", received, expert_up, preferred_element_type=jnp.float32
    )
    routed_hidden = (gate_routed * sigmoid(gate_routed) * up_routed).astype(jnp.bfloat16)
    routed_part = jnp.einsum(
        "secf,efd->secd", routed_hidden, expert_down, preferred_element_type=jnp.float32
    ).astype(jnp.bfloat16)
    combined = lax.all_to_all(
        routed_part, "expert", split_axis=0, concat_axis=0, tiled=True
    ).reshape(experts * capacity, D)
    returned = combined[flat_rows].astype(jnp.float32).reshape(length, TOP, D)
    routed_sum = jnp.sum(returned * mixing[:, :, None], axis=1)
    mixture = lax.psum((shared_part + routed_sum).astype(jnp.bfloat16), "tensor").astype(
        jnp.float32
    )
    block_output = (middle + mixture).astype(jnp.bfloat16)
    upstream = cotangent.astype(jnp.float32)
    shared_gate_grad, shared_up_grad = swiglu_backward(
        matmul_nt(cotangent, common_down), gate_pre, up_pre
    )
    common_down_grad = matmul_tn(shared_hidden, cotangent)
    common_gate_grad = matmul_tn(normed_mid, shared_gate_grad)
    common_up_grad = matmul_tn(normed_mid, shared_up_grad)
    grad_mid_partial = matmul_nt(shared_gate_grad, common_gate) + matmul_nt(
        shared_up_grad, common_up
    )
    outgoing_grad = (
        (mixing[:, :, None] * upstream[:, None, :]).astype(jnp.bfloat16).reshape(length * TOP, D)
    )
    grad_outgoing = (
        jnp.zeros((experts * capacity, D), jnp.bfloat16)
        .at[flat_rows]
        .set(outgoing_grad)
        .reshape(groups, local_experts, capacity, D)
    )
    grad_received = lax.all_to_all(grad_outgoing, "expert", split_axis=0, concat_axis=0, tiled=True)
    grad_routed_hidden = jnp.einsum(
        "secd,efd->secf", grad_received, expert_down, preferred_element_type=jnp.float32
    )
    routed_gate_grad, routed_up_grad = swiglu_backward(grad_routed_hidden, gate_routed, up_routed)
    expert_down_grad = jnp.einsum(
        "secf,secd->efd", routed_hidden, grad_received, preferred_element_type=jnp.float32
    )
    expert_gate_grad = jnp.einsum(
        "secd,secf->edf", received, routed_gate_grad, preferred_element_type=jnp.float32
    )
    expert_up_grad = jnp.einsum(
        "secd,secf->edf", received, routed_up_grad, preferred_element_type=jnp.float32
    )
    grad_input_rows = (
        jnp.einsum(
            "secf,edf->secd", routed_gate_grad, expert_gate, preferred_element_type=jnp.float32
        )
        + jnp.einsum(
            "secf,edf->secd", routed_up_grad, expert_up, preferred_element_type=jnp.float32
        )
    ).astype(jnp.bfloat16)
    sent_back = lax.all_to_all(
        grad_input_rows, "expert", split_axis=0, concat_axis=0, tiled=True
    ).reshape(experts * capacity, D)
    back_rows = sent_back[flat_rows].astype(jnp.float32).reshape(length, TOP, D)
    grad_mid_partial = grad_mid_partial + jnp.sum(back_rows, axis=1)
    mixing_partial = jnp.sum(returned * upstream[:, None, :], axis=2)
    grad_mid_sum, grad_mixing = (
        lax.psum(grad_mid_partial.astype(jnp.bfloat16), "tensor").astype(jnp.float32),
        lax.psum(mixing_partial.astype(jnp.bfloat16), "tensor").astype(jnp.float32),
    )
    grad_selected = ROUTE_SCALE * (
        grad_mixing / selected_total
        - jnp.sum(grad_mixing * selected, axis=1, keepdims=True) / (selected_total * selected_total)
    )
    grad_affinity = jnp.sum(onehot * grad_selected[:, :, None], axis=1)
    grad_logits = (grad_affinity * affinity * (1.0 - affinity)).astype(jnp.bfloat16)
    router_grad = matmul_tn(normed_mid, grad_logits)
    grad_mid_sum = grad_mid_sum + matmul_nt(grad_logits, router_full)
    grad_middle_norm, post_grad = norm_backward(grad_mid_sum, middle, inverse_post, post_gain)
    grad_middle = upstream + grad_middle_norm
    grad_attention = grad_middle.astype(jnp.bfloat16)
    output_grad = matmul_tn(attended, grad_attention)
    grad_attended = (
        matmul_nt(grad_attention, output_full).astype(jnp.bfloat16).reshape(length, heads, HEAD_DIM)
    )
    probabilities = jnp.exp(score_block() - log_total)
    grad_probs = jnp.einsum(
        "qhd,khd->hqk", grad_attended, values, preferred_element_type=jnp.float32
    )
    inner = jnp.sum(probabilities * grad_probs, axis=2, keepdims=True)
    grad_scores = (probabilities * (grad_probs - inner)).astype(jnp.bfloat16)
    grad_query_nope = scale * jnp.einsum(
        "hqk,khd->qhd", grad_scores, key_nope, preferred_element_type=jnp.float32
    )
    grad_query_rope = scale * jnp.einsum(
        "hqk,kr->qhr", grad_scores, key_rope, preferred_element_type=jnp.float32
    )
    grad_key_nope = scale * jnp.einsum(
        "hqk,qhd->khd", grad_scores, query_nope, preferred_element_type=jnp.float32
    )
    grad_key_rope = scale * jnp.einsum(
        "hqk,qhr->kr", grad_scores, query_rope, preferred_element_type=jnp.float32
    )
    grad_values = jnp.einsum(
        "hqk,qhd->khd",
        probabilities.astype(jnp.bfloat16),
        grad_attended,
        preferred_element_type=jnp.float32,
    )
    grad_query = (
        jnp.concatenate(
            [grad_query_nope, rotate(grad_query_rope, cosine[:, None, :], -sine[:, None, :])],
            axis=2,
        )
        .astype(jnp.bfloat16)
        .reshape(length, heads * (HEAD_DIM + ROPE_DIM))
    )
    query_grad = matmul_tn(normed, grad_query)
    grad_expanded = (
        jnp.concatenate([grad_key_nope, grad_values], axis=2)
        .astype(jnp.bfloat16)
        .reshape(length, heads * 2 * HEAD_DIM)
    )
    expand_grad = matmul_tn(compressed, grad_expanded)
    grad_normed_sum, grad_compressed, grad_key_raw = (
        lax.psum(matmul_nt(grad_query, query_full).astype(jnp.bfloat16), "tensor").astype(
            jnp.float32
        ),
        lax.psum(matmul_nt(grad_expanded, expand_full).astype(jnp.bfloat16), "tensor").astype(
            jnp.float32
        ),
        lax.psum(rotate(grad_key_rope, cosine, -sine).astype(jnp.bfloat16), "tensor").astype(
            jnp.float32
        ),
    )
    grad_latent_raw, latent_norm_grad = norm_backward(
        grad_compressed, latent_raw, inverse_latent, latent_gain
    )
    grad_latent = jnp.concatenate([grad_latent_raw, grad_key_raw], axis=1).astype(jnp.bfloat16)
    latent_grad = matmul_tn(normed, grad_latent)
    grad_normed = grad_normed_sum + matmul_nt(grad_latent, latent_full)
    grad_hidden, pre_grad = norm_backward(grad_normed, hidden, inverse_pre, pre_gain)
    input_gradient = (grad_middle + grad_hidden).astype(jnp.bfloat16)
    (
        query_out,
        latent_out,
        expand_out,
        output_out,
        pre_out,
        latent_norm_out,
        post_out,
        router_out,
        gate_out,
        up_out,
        down_out,
    ) = (
        lax.psum_scatter(
            query_grad.astype(jnp.bfloat16), "expert", scatter_dimension=0, tiled=True
        ).astype(jnp.float32),
        lax.psum_scatter(
            latent_grad.astype(jnp.bfloat16), "expert", scatter_dimension=0, tiled=True
        ).astype(jnp.float32),
        lax.psum_scatter(
            expand_grad.astype(jnp.bfloat16), "expert", scatter_dimension=0, tiled=True
        ).astype(jnp.float32),
        lax.psum_scatter(
            output_grad.astype(jnp.bfloat16), "expert", scatter_dimension=1, tiled=True
        ).astype(jnp.float32),
        lax.psum_scatter(
            pre_grad.astype(jnp.bfloat16), "expert", scatter_dimension=0, tiled=True
        ).astype(jnp.float32),
        lax.psum_scatter(
            latent_norm_grad.astype(jnp.bfloat16), "expert", scatter_dimension=0, tiled=True
        ).astype(jnp.float32),
        lax.psum_scatter(
            post_grad.astype(jnp.bfloat16), "expert", scatter_dimension=0, tiled=True
        ).astype(jnp.float32),
        lax.psum_scatter(
            router_grad.astype(jnp.bfloat16), "expert", scatter_dimension=0, tiled=True
        ).astype(jnp.float32),
        lax.psum_scatter(
            common_gate_grad.astype(jnp.bfloat16), "expert", scatter_dimension=0, tiled=True
        ).astype(jnp.float32),
        lax.psum_scatter(
            common_up_grad.astype(jnp.bfloat16), "expert", scatter_dimension=0, tiled=True
        ).astype(jnp.float32),
        lax.psum_scatter(
            common_down_grad.astype(jnp.bfloat16), "expert", scatter_dimension=1, tiled=True
        ).astype(jnp.float32),
    )
    return (
        block_output,
        input_gradient,
        query_out,
        latent_out,
        expand_out,
        output_out,
        pre_out,
        latent_norm_out,
        post_out,
        router_out,
        gate_out,
        up_out,
        down_out,
        expert_gate_grad,
        expert_up_grad,
        expert_down_grad,
    )


def solution(mesh):
    placed = (
        P("expert", None),
        P("expert", None),
        P("expert", None),
        P("expert", "tensor"),
        P("expert", None),
        P("expert", "tensor"),
        P("tensor", "expert"),
        P("expert"),
        P("expert"),
        P("expert"),
        P("expert", None),
        P("expert", "tensor"),
        P("expert", "tensor"),
        P("tensor", "expert"),
        P("expert", None, "tensor"),
        P("expert", None, "tensor"),
        P("expert", "tensor", None),
        P("expert", None),
    )
    return jax.shard_map(
        shards,
        mesh=mesh,
        in_specs=placed,
        out_specs=(
            P("expert", None),
            P("expert", None),
            P("expert", "tensor"),
            P("expert", None),
            P("expert", "tensor"),
            P("tensor", "expert"),
            P("expert"),
            P("expert"),
            P("expert"),
            P("expert", None),
            P("expert", "tensor"),
            P("expert", "tensor"),
            P("tensor", "expert"),
            P("expert", None, "tensor"),
            P("expert", None, "tensor"),
            P("expert", "tensor", None),
        ),
        check_vma=False,
    )
```

profile of v0, /device:TPU:0, one launch (start us, length us, event | category | flops | bytes accessed | tf_op | source)
XLA Modules:
  0.0 1386.4 jit_solution(17128408199766225182)
XLA Ops:
  14.1 15.2 %all-reduce = bf16[512]{0:T(512)(128)(2,1)S(1)} all-reduce(bf16[512]{0:T(512)(128)(2,1)S(1)} %dynamic-update-slice), channel_id=1, replica_groups=mesh['expert'=8,'tensor'=4] {'expert'}, use_global_device_ids=true, to_apply=%add | all-reduce | flops 512 | bytes 2048
  29.4 8.1 all-gather
  45.0 22.3 %all-gather.12.cloned.1.call-done = bf16[512,1024]{1,0:T(8,128)(2,1)} async-done(((bf16[64,1024]{1,0:T(8,128)(2,1)}), bf16[512,1024]{1,0:T(8,128)(2,1)}) %all-gather.12.cloned.1.call-update) | async-done | bytes 1048592 | tf_op jit(solution)/shard_map/all_gather | solution.py:123
  77.3 24.0 %all-gather.14.cloned.1.call-done = bf16[2048,768]{1,0:T(8,128)(2,1)} async-done(((bf16[256,768]{1,0:T(8,128)(2,1)}), bf16[2048,768]{1,0:T(8,128)(2,1)}) %all-gather.14.cloned.1.call-update) | async-done | bytes 3145744 | tf_op jit(solution)/shard_map/all_gather | solution.py:121
  107.9 23.3 %all-gather.16.cloned.1.call-done = bf16[512,2048]{1,0:T(8,128)(2,1)} async-done(((bf16[512,256]{1,0:T(8,128)(2,1)}), bf16[512,2048]{1,0:T(8,128)(2,1)}) %all-gather.16.cloned.1.call-update) | async-done | bytes 2097168 | tf_op jit(solution)/shard_map/all_gather | solution.py:124
  135.4 9.1 all-gather.1
  150.4 70.9 %all-reduce.10.cloned.1.call-done = f32[256,2048]{1,0:T(8,128)} async-done(((f32[256,2048]{1,0:T(8,128)}), f32[256,2048]{1,0:T(8,128)}) %all-reduce.10.cloned.1.call-update) | async-done | bytes 2097168 | tf_op jit(solution)/shard_map/psum | solution.py:186
  226.0 5.9 broadcast_in_dim.20
  231.9 11.0 reshape.382
  242.9 17.5 %scatter_custom_fusion = bf16[3072,2048]{1,0:T(8,128)(2,1)} fusion(s32[1536]{0:T(1024)S(1)} %fusion.103, bf16[1536,2048]{1,0:T(8,128)(2,1)} %reshape.382, bf16[]{:T(256)} %constant.13.clone.1), kind=kCustom, calls=%fused_computation.21 | custom fusion | bytes 12583424 | tf_op jit(solution)/shard_map/scatter | solution.py:206
  260.4 5.4 all-to-all-start
  265.8 9.1 mul.667
  274.9 15.7 %mul.668 = f32[1536,2048]{1,0:T(8,128)} reshape(f32[256,6,2048]{2,1,0:T(8,128)} %mul.667) | data formatting | bytes 25165824 | tf_op jit(solution)/shard_map/mul | solution.py:240
  290.7 117.3 %all_gather.43 = bf16[2048,16]{0,1:T(8,128)(2,1)S(1)} all-gather(bf16[256,16]{0,1:T(8,128)(2,1)S(1)} %copy-done.70), channel_id=1, replica_groups=mesh['expert'=8,'tensor'=4] {'expert'}, dimensions={0}, use_global_device_ids=true | all-gather | bytes 73728 | tf_op jit(solution)/shard_map/all_gather | solution.py:128
  410.6 18.3 %scatter_custom_fusion.1 = bf16[3072,2048]{1,0:T(8,128)(2,1)} fusion(s32[1536]{0:T(1024)S(1)} %fusion.103, f32[1536,2048]{1,0:T(8,128)} %mul.668, f32[1536]{0:T(1024)S(1)} %div.77, bf16[]{:T(256)} %constant.13.clone.1), kind=kCustom, calls=%fused_computation.18 | custom fusion | flops 6291456 | bytes 25174018 | tf_op jit(solution)/shard_map/scatter | solution.py:245
  428.9 5.3 all-to-all-start.2
  434.9 12.0 fusion.5
  446.9 11.2 fusion.7
  458.1 126.7 %all-to-all-done.2 = bf16[8,2,192,2048]{3,2,1,0:T(8,128)(2,1)} async-done(((bf16[8,2,192,2048]{3,2,1,0:T(8,128)(2,1)}), bf16[8,2,192,2048]{3,2,1,0:T(8,128)(2,1)}, u32[]{:S(2)}, u32[]{:S(2)}) %all-to-all-start.2) | async-done | bytes 12582944 | tf_op jit(solution)/shard_map/all_to_all | solution.py:248
  584.8 14.7 %fusion.18 = (bf16[8,2,192,352]{3,2,0,1:T(8,128)(2,1)}, bf16[8,2,192,352]{3,2,0,1:T(8,128)(2,1)S(1)}, bf16[8,2,192,352]{3,2,0,1:T(8,128)(2,1)}) fusion(f32[2,8,192,352]{3,2,1,0:T(8,128)} %fusion.7, f32[2,8,192,352]{3,2,1,0:T(8,128)} %fusion.5, bf16[2,352,2048]{2,1,0:T(8,128)(2,1)S(1)} %copy-done, bf16[8,2,192,2048]{3,2,1,0:T(8,128)(2,1)} %all-to-all-done.2), kind=kOutput, calls=%fused_computation.29 | convolution fusion | flops 4446486528 | bytes 30605312 | tf_op jit(solution)/shard_map/secd,efd->secf/dot_general | solution.py:249
  599.5 12.0 fusion.29
  611.5 15.7 %fusion = bf16[8,2,192,2048]{3,2,0,1:T(8,128)(2,1)} fusion(f32[2,8,192,2048]{3,2,1,0:T(8,128)} %fusion.29, bf16[8,2,192,352]{3,2,0,1:T(8,128)(2,1)} %get-tuple-element.34, bf16[2,2048,352]{1,2,0:T(8,128)(2,1)} %param.33), kind=kOutput, calls=%fused_computation.7 | convolution fusion | flops 4441767936 | bytes 42795008 | tf_op jit(solution)/shard_map/secf,edf->secd/dot_general | solution.py:266
  627.2 10.8 copy.185
  637.9 5.4 all-to-all-start.3
  648.8 87.5 %all-gather.18.cloned.1.call-done = bf16[2048,704]{0,1:T(8,128)(2,1)} async-done(((bf16[256,704]{0,1:T(8,128)(2,1)}), bf16[2048,704]{0,1:T(8,128)(2,1)}) %all-gather.18.cloned.1.call-update) | async-done | bytes 2883600 | tf_op jit(solution)/shard_map/all_gather | solution.py:129
  740.4 6.9 convert_bitcast_fusion
  752.6 52.9 %all-to-all-done.3 = bf16[8,2,192,2048]{3,2,1,0:T(8,128)(2,1)} async-done(((bf16[8,2,192,2048]{3,2,1,0:T(8,128)(2,1)}), bf16[8,2,192,2048]{3,2,1,0:T(8,128)(2,1)}, u32[]{:S(2)}, u32[]{:S(2)}) %all-to-all-start.3) | async-done | bytes 12582944 | tf_op jit(solution)/shard_map/all_to_all | solution.py:270
  805.5 5.4 all-to-all-start.1
  817.0 18.9 %gather_fusion.1 = bf16[1536,2048]{1,0:T(8,128)(2,1)} fusion(bf16[3072,2048]{1,0:T(8,128)(2,1)} %bitcast.27, s32[2048]{0:T(1024)S(1)} %pad_clamp_fusion), kind=kCustom, calls=%fused_computation.1 | custom fusion | bytes 12589056 | tf_op jit(solution)/shard_map/gather | solution.py:273
  835.9 11.7 reshape.361
  847.6 9.8 reduce_sum.179
  872.1 85.5 %all-to-all-done.1 = bf16[8,2,192,2048]{3,2,1,0:T(8,128)(2,1)} async-done(((bf16[8,2,192,2048]{3,2,1,0:T(8,128)(2,1)}), bf16[8,2,192,2048]{3,2,1,0:T(8,128)(2,1)}, u32[]{:S(2)}, u32[]{:S(2)}) %all-to-all-start.1) | async-done | bytes 12582944 | tf_op jit(solution)/shard_map/all_to_all | solution.py:220
  957.6 19.2 %gather_fusion = bf16[1536,2048]{1,0:T(8,128)(2,1)} fusion(bf16[3072,2048]{1,0:T(8,128)(2,1)} %bitcast.20, s32[2048]{0:T(1024)S(1)} %pad_clamp_fusion), kind=kCustom, calls=%fused_computation | custom fusion | bytes 12589056 | tf_op jit(solution)/shard_map/gather | solution.py:223
  976.8 12.2 reshape.360
  989.1 12.1 multiply_reduce_fusion
  1001.2 9.4 psum.52
  1046.7 19.1 %reduce-scatter.23.cloned.1.call-done = bf16[704,256]{1,0:T(8,128)(2,1)} async-done(((bf16[704,2048]{1,0:T(8,128)(2,1)}), bf16[704,256]{1,0:T(8,128)(2,1)}) %reduce-scatter.23.cloned.1.call-update) | async-done | bytes 360464 | tf_op jit(solution)/shard_map/reduce_scatter | solution.py:396
  1067.8 10.0 convolution_bitcast_fusion
  1077.8 20.9 %psum.55 = bf16[256,64]{0,1:T(8,128)(2,1)S(1)} all-reduce(bf16[256,64]{0,1:T(8,128)(2,1)S(1)} %pad_maximum_fusion.8), channel_id=1, replica_groups=mesh['expert'=8,'tensor'=4] {'tensor'}, use_global_device_ids=true, to_apply=%region_26.27 | all-reduce | flops 16384 | bytes 65536 | tf_op jit(solution)/shard_map/psum | solution.py:341
  1098.7 66.1 %all-reduce.14.cloned.1.call-done = (bf16[256,2048]{1,0:T(8,128)(2,1)}, bf16[256,2048]{1,0:T(8,128)(2,1)}, bf16[256,512]{0,1:T(8,128)(2,1)}) async-done(((bf16[256,2048]{1,0:T(8,128)(2,1)}, bf16[256,2048]{1,0:T(8,128)(2,1)}, bf16[256,512]{0,1:T(8,128)(2,1)}), (bf16[256,2048]{1,0:T(8,128)(2,1)}, bf16[256,2048]{1,0:T(8,128)(2,1)}, bf16[256,512]{0,1:T(8,128)(2,1)})) %all-reduce.14.cloned.1.call-update) | async-done | bytes 2359312 | tf_op jit(solution)/shard_map/psum | solution.py:225
  1170.8 10.1 convolution_bitcast_fusion.1
  1180.9 10.4 fusion.24
  1191.3 7.4 reduce-scatter.17.cloned.1.call-done
  1200.0 38.3 %reduce-scatter.13.cloned.1.call-done = bf16[64,1024]{1,0:T(8,128)(2,1)} async-done(((bf16[512,1024]{1,0:T(8,128)(2,1)}), bf16[64,1024]{1,0:T(8,128)(2,1)}) %reduce-scatter.13.cloned.1.call-update) | async-done | bytes 131088 | tf_op jit(solution)/shard_map/reduce_scatter | solution.py:372
  1244.9 12.8 all-reduce.4
  1264.9 17.7 %reduce-scatter.15.cloned.1.call-done = bf16[512,256]{1,0:T(8,128)(2,1)} async-done(((bf16[512,2048]{1,0:T(8,128)(2,1)}), bf16[512,256]{1,0:T(8,128)(2,1)}) %reduce-scatter.15.cloned.1.call-update) | async-done | bytes 262160 | tf_op jit(solution)/shard_map/reduce_scatter | solution.py:375
  1284.4 47.5 %reduce-scatter.9.cloned.1.call-done = bf16[256,768]{1,0:T(8,128)(2,1)} async-done(((bf16[2048,768]{1,0:T(8,128)(2,1)}), bf16[256,768]{1,0:T(8,128)(2,1)}) %reduce-scatter.9.cloned.1.call-update) | async-done | bytes 393232 | tf_op jit(solution)/shard_map/reduce_scatter | solution.py:366
  1333.8 43.6 %reduce-scatter.11.cloned.1.call-done = bf16[256,576]{0,1:T(8,128)(2,1)} async-done(((bf16[2048,576]{0,1:T(8,128)(2,1)}), bf16[256,576]{0,1:T(8,128)(2,1)}) %reduce-scatter.11.cloned.1.call-update) | async-done | bytes 294928 | tf_op jit(solution)/shard_map/reduce_scatter | solution.py:369
  (312 shorter events, 146.0 us)
Async XLA Ops:
  7.2 577.7 %copy-start = (bf16[2,352,2048]{2,1,0:T(8,128)(2,1)S(1)}, bf16[2,352,2048]{2,1,0:T(8,128)(2,1)}, u32[]{:S(2)}) copy-start(bf16[2,352,2048]{2,1,0:T(8,128)(2,1)} %param.34) | copy-start | bytes 8650756
  7.2 34.8 %all-gather.10.cloned.1.call-start = ((), (), s32[]{:S(2)}) async-start(), calls=%async_computation.12 | async-start | bytes 2654208 | tf_op jit(solution)/shard_map/all_gather | solution.py:122
  7.9 59.3 %all-gather.12.cloned.1.call-start = ((), (), s32[]{:S(2)}) async-start(), calls=%async_computation.13 | async-start | bytes 1179648 | tf_op jit(solution)/shard_map/all_gather | solution.py:123
  8.7 92.7 %all-gather.14.cloned.1.call-start = ((), (), s32[]{:S(2)}) async-start(), calls=%async_computation.14 | async-start | bytes 3538944 | tf_op jit(solution)/shard_map/all_gather | solution.py:121
  9.4 121.8 %all-gather.16.cloned.1.call-start = ((), (), s32[]{:S(2)}) async-start(), calls=%async_computation.15 | async-start | bytes 2359296 | tf_op jit(solution)/shard_map/all_gather | solution.py:124
  10.0 211.2 %all-reduce.10.cloned.1.call-start = ((), (), s32[]{:S(2)}) async-start(), calls=%async_computation.16 | async-start | bytes 4194304 | tf_op jit(solution)/shard_map/psum | solution.py:186
  10.0 65.8 %copy-start.71 = (f32[256]{0:T(256)}, f32[256]{0:T(256)S(1)}, u32[]{:S(2)}) copy-start(f32[256]{0:T(256)S(1)} %iota_convert_fusion) | copy-start | bytes 3076
  29.4 37.9 %copy-start.58 = (f32[512]{0:T(512)}, f32[512]{0:T(512)S(1)}, u32[]{:S(2)}) copy-start(f32[512]{0:T(512)S(1)} %convert_element_type.306) | copy-start | bytes 6148
  37.5 63.8 %copy-start.38 = (f32[8,1,256]{2,1,0:T(1,128)}, f32[8,1,256]{2,1,0:T(1,128)S(1)}, u32[]{:S(2)}) copy-start(f32[8,1,256]{2,1,0:T(1,128)S(1)} %convert_element_type.377) | copy-start | bytes 24580
  39.1 62.3 %copy-start.56 = (f32[256]{0:T(256)}, f32[256]{0:T(256)S(1)}, u32[]{:S(2)}) copy-start(f32[256]{0:T(256)S(1)} %add_rsqrt_fusion.2) | copy-start | bytes 3076
  44.8 60.2 %copy-start.11 = (f32[256,576]{0,1:T(8,128)}, f32[256,576]{0,1:T(8,128)S(1)}, u32[]{:S(2)}) copy-start(f32[256,576]{0,1:T(8,128)S(1)} %fusion.113) | copy-start | bytes 1769476
  45.0 29.1 %copy-start.62 = (f32[256]{0:T(256)}, f32[256]{0:T(256)S(1)}, u32[]{:S(2)}) copy-start(f32[256]{0:T(256)S(1)} %add_rsqrt_fusion.1) | copy-start | bytes 3076
  77.3 27.8 %copy-start.40 = (f32[256,32]{0,1:T(8,128)}, f32[256,32]{0,1:T(8,128)S(1)}, u32[]{:S(2)}) copy-start(f32[256,32]{0,1:T(8,128)S(1)} %get-tuple-element.52) | copy-start | bytes 98308
  77.3 28.2 %copy-start.43 = (bf16[256,32]{0,1:T(8,128)(2,1)}, bf16[256,32]{0,1:T(8,128)(2,1)S(1)}, u32[]{:S(2)}) copy-start(bf16[256,32]{0,1:T(8,128)(2,1)S(1)} %get-tuple-element.42) | copy-start | bytes 49156
  77.3 28.2 %copy-start.45 = (bf16[256,32]{0,1:T(8,128)(2,1)}, bf16[256,32]{0,1:T(8,128)(2,1)S(1)}, u32[]{:S(2)}) copy-start(bf16[256,32]{0,1:T(8,128)(2,1)S(1)} %get-tuple-element.43) | copy-start | bytes 49156
  105.9 28.9 %copy-start.60 = (f32[4,256]{1,0:T(4,128)}, f32[4,256]{1,0:T(4,128)S(1)}, u32[]{:S(2)}) copy-start(f32[4,256]{1,0:T(4,128)S(1)} %get-tuple-element.55) | copy-start | bytes 12292
  107.9 27.0 %copy-start.28 = (bf16[4,128,256]{2,1,0:T(8,128)(2,1)}, bf16[4,128,256]{2,1,0:T(8,128)(2,1)S(1)}, u32[]{:S(2)}) copy-start(bf16[4,128,256]{2,1,0:T(8,128)(2,1)S(1)} %convolution_convert_fusion.13) | copy-start | bytes 786436
  144.4 79.0 %copy-start.49 = (f32[8,1,256]{2,1,0:T(1,128)}, f32[8,1,256]{2,1,0:T(1,128)S(1)}, u32[]{:S(2)}) copy-start(f32[8,1,256]{2,1,0:T(1,128)S(1)} %convert_element_type.378) | copy-start | bytes 24580
  260.4 168.5 %all-to-all-start = ((bf16[8,2,192,2048]{3,2,1,0:T(8,128)(2,1)}), bf16[8,2,192,2048]{3,2,1,0:T(8,128)(2,1)}, u32[]{:S(2)}, u32[]{:S(2)}) async-start(bf16[8,2,192,2048]{3,2,1,0:T(8,128)(2,1)} %bitcast.189), calls=%async_computation | async-start | bytes 25165824 | tf_op jit(solution)/shard_map/all_to_all | solution.py:209
  274.9 15.7 %copy-start.70 = (bf16[256,16]{0,1:T(8,128)(2,1)S(1)}, bf16[256,16]{0,1:T(8,128)(2,1)}, u32[]{:S(2)}) copy-start(bf16[256,16]{0,1:T(8,128)(2,1)} %param.28) | copy-start | bytes 24580
  409.7 19.2 %copy-start.66 = (f32[256]{0:T(256)}, f32[256]{0:T(256)S(1)}, u32[]{:S(2)}) copy-start(f32[256]{0:T(256)S(1)} %get-tuple-element.24) | copy-start | bytes 3076
  410.4 18.5 %copy-start.26 = (f32[256,6]{1,0:T(8,128)}, f32[256,6]{1,0:T(8,128)S(1)}, u32[]{:S(2)}) copy-start(f32[256,6]{1,0:T(8,128)S(1)} %copy.182) | copy-start | bytes 18436
  428.9 155.9 %all-to-all-start.2 = ((bf16[8,2,192,2048]{3,2,1,0:T(8,128)(2,1)}), bf16[8,2,192,2048]{3,2,1,0:T(8,128)(2,1)}, u32[]{:S(2)}, u32[]{:S(2)}) async-start(bf16[8,2,192,2048]{3,2,1,0:T(8,128)(2,1)} %bitcast.190), calls=%async_computation.2 | async-start | bytes 25165824 | tf_op jit(solution)/shard_map/all_to_all | solution.py:248
  434.3 210.6 %all-gather.20.cloned.1.call-start = ((), (), s32[]{:S(2)}) async-start(), calls=%async_computation.18 | async-start | bytes 3244032 | tf_op jit(solution)/shard_map/all_gather | solution.py:130
  584.8 14.7 %copy-start.19 = (bf16[2,2048,352]{1,2,0:T(8,128)(2,1)S(1)}, bf16[2,2048,352]{1,2,0:T(8,128)(2,1)}, u32[]{:S(2)}) copy-start(bf16[2,2048,352]{1,2,0:T(8,128)(2,1)} %param.32) | copy-start | bytes 8650756
  637.9 167.5 %all-to-all-start.3 = ((bf16[8,2,192,2048]{3,2,1,0:T(8,128)(2,1)}), bf16[8,2,192,2048]{3,2,1,0:T(8,128)(2,1)}, u32[]{:S(2)}, u32[]{:S(2)}) async-start(bf16[8,2,192,2048]{3,2,1,0:T(8,128)(2,1)} %copy.185), calls=%async_computation.3 | async-start | bytes 25165824 | tf_op jit(solution)/shard_map/all_to_all | solution.py:270
  643.3 93.0 %all-gather.18.cloned.1.call-start = ((), (), s32[]{:S(2)}) async-start(), calls=%async_computation.17 | async-start | bytes 3244032 | tf_op jit(solution)/shard_map/all_gather | solution.py:129
  644.1 167.3 %all-gather.22.cloned.1.call-start = ((), (), s32[]{:S(2)}) async-start(), calls=%async_computation.19 | async-start | bytes 3244032 | tf_op jit(solution)/shard_map/all_gather | solution.py:131
  752.6 58.8 %copy-start.9 = (bf16[256,2048]{1,0:T(8,128)(2,1)S(1)}, bf16[256,2048]{1,0:T(8,128)(2,1)}, u32[]{:S(2)}) copy-start(bf16[256,2048]{1,0:T(8,128)(2,1)} %param.35) | copy-start | bytes 3145732
  752.6 58.8 %copy-start.76 = (f32[256,704]{0,1:T(8,128)S(1)}, f32[256,704]{0,1:T(8,128)}, u32[]{:S(2)}) copy-start(f32[256,704]{0,1:T(8,128)} %fusion.120) | copy-start | bytes 2162692
  805.5 152.1 %all-to-all-start.1 = ((bf16[8,2,192,2048]{3,2,1,0:T(8,128)(2,1)}), bf16[8,2,192,2048]{3,2,1,0:T(8,128)(2,1)}, u32[]{:S(2)}, u32[]{:S(2)}) async-start(bf16[8,2,192,2048]{3,2,1,0:T(8,128)(2,1)} %copy.181), calls=%async_computation.1 | async-start | bytes 25165824 | tf_op jit(solution)/shard_map/all_to_all | solution.py:220
  810.9 204.5 %all-reduce.12.cloned.1.call-start = ((), (), s32[]{:S(2)}) async-start(), calls=%async_computation.20 | async-start | bytes 2097152 | tf_op jit(solution)/shard_map/psum | solution.py:277
  862.6 180.3 %reduce-scatter.21.cloned.1.call-start = ((), (), s32[]{:S(2)}) async-start(), calls=%async_computation.27 | async-start | bytes 3244032 | tf_op jit(solution)/shard_map/reduce_scatter | solution.py:393
  865.2 179.7 %reduce-scatter.19.cloned.1.call-start = ((), (), s32[]{:S(2)}) async-start(), calls=%async_computation.26 | async-start | bytes 3244032 | tf_op jit(solution)/shard_map/reduce_scatter | solution.py:390
  867.8 198.1 %reduce-scatter.23.cloned.1.call-start = ((), (), s32[]{:S(2)}) async-start(), calls=%async_computation.28 | async-start | bytes 3244032 | tf_op jit(solution)/shard_map/reduce_scatter | solution.py:396
  872.0 292.8 %all-reduce.14.cloned.1.call-start = ((), (), s32[]{:S(2)}) async-start(), calls=%async_computation.29 | async-start | bytes 4718592 | tf_op jit(solution)/shard_map/psum | solution.py:225
  976.8 12.2 copy-start.14
  976.8 12.2 copy-start.27
  989.0 21.6 %copy-start.55 = (f32[256,6]{0,1:T(8,128)S(1)}, f32[256,6]{0,1:T(8,128)}, u32[]{:S(2)}) copy-start(f32[256,6]{0,1:T(8,128)} %copy-done.54) | copy-start | bytes 18436
  989.0 21.6 %copy-start.67 = (f32[256]{0:T(256)S(1)}, f32[256]{0:T(256)}, u32[]{:S(2)}) copy-start(f32[256]{0:T(256)} %copy-done.66) | copy-start | bytes 3076
  989.0 21.7 %copy-start.53 = (s32[256,6]{0,1:T(8,128)S(1)}, s32[256,6]{0,1:T(8,128)}, u32[]{:S(2)}) copy-start(s32[256,6]{0,1:T(8,128)} %param.20) | copy-start | bytes 18436
  989.0 21.7 %copy-start.48 = (f32[256,16]{0,1:T(8,128)S(1)}, f32[256,16]{0,1:T(8,128)}, u32[]{:S(2)}) copy-start(f32[256,16]{0,1:T(8,128)} %copy-done.47) | copy-start | bytes 49156
  1029.6 169.1 %reduce-scatter.17.cloned.1.call-start = ((), (), s32[]{:S(2)}) async-start(), calls=%async_computation.25 | async-start | bytes 73728 | tf_op jit(solution)/shard_map/reduce_scatter | solution.py:387
  1032.0 206.3 %reduce-scatter.13.cloned.1.call-start = ((), (), s32[]{:S(2)}) async-start(), calls=%async_computation.23 | async-start | bytes 1179648 | tf_op jit(solution)/shard_map/reduce_scatter | solution.py:372
  1033.6 249.0 %reduce-scatter.15.cloned.1.call-start = ((), (), s32[]{:S(2)}) async-start(), calls=%async_computation.24 | async-start | bytes 2359296 | tf_op jit(solution)/shard_map/reduce_scatter | solution.py:375
  1037.5 294.4 %reduce-scatter.9.cloned.1.call-start = ((), (), s32[]{:S(2)}) async-start(), calls=%async_computation.21 | async-start | bytes 3538944 | tf_op jit(solution)/shard_map/reduce_scatter | solution.py:366
  1041.6 335.9 %reduce-scatter.11.cloned.1.call-start = ((), (), s32[]{:S(2)}) async-start(), calls=%async_computation.22 | async-start | bytes 2654208 | tf_op jit(solution)/shard_map/reduce_scatter | solution.py:369
  1261.5 117.8 %copy-start.1 = (bf16[2,352,2048]{2,1,0:T(8,128)(2,1)S(1)}, bf16[2,352,2048]{2,1,0:T(8,128)(2,1)}, u32[]{:S(2)}) copy-start(bf16[2,352,2048]{2,1,0:T(8,128)(2,1)} %param.34) | copy-start | bytes 8650756
  (53 other events, 171.5 us)
Sparse Core Ops, SparseCore 0:
  9.9 32.0 all-gather.9
  43.8 23.3 all-gather.11
  69.1 32.1 all-gather.13
  103.1 28.0 all-gather.15
  135.0 86.1 all-reduce.9
  436.6 90.5 all-gather.19
  646.0 90.2 all-gather.17
  738.2 53.1 all-gather.21
  862.7 51.4 all-reduce.11
  918.1 50.4 reduce-scatter.20
  972.6 44.7 reduce-scatter.18
  1021.1 44.6 reduce-scatter.22
  1069.0 95.7 all-reduce.13
  1168.3 30.3 reduce-scatter.16
  1202.3 35.9 reduce-scatter.12
  1241.4 41.1 reduce-scatter.14
  1285.8 46.0 reduce-scatter.8
  1335.1 42.3 reduce-scatter.10
where the time goes:
time: 1390 us
  waiting for transfers between devices  739 us (53%)
  blocking collectives  193 us (14%)
  matrix products  179 us (13%)
  local copies, waits for them, and re-layouts  154 us (11%)
  other arithmetic  82 us (6%)
  starting transfers between devices  23.1 us (2%)
  between operations  17.7 us (1%)
    all_to_all x1, waiting for transfers between devices, shards(): lax.all_to_all(grad_outgoing, 'expert', split_axis=0, concat_axis=0, tile...  127 us
    all_gather x1, blocking collectives, shards(): lax.all_gather(router_weight, 'expert', axis=0, tiled=True)  117 us
    all_gather x1, waiting for transfers between devices, shards(): lax.all_gather(shared_gate, 'expert', axis=0, tiled=True)  87.5 us
    all_to_all x1, waiting for transfers between devices, shards(): lax.all_to_all(routed_part, 'expert', split_axis=0, concat_axis=0, tiled=...  85.5 us
    psum x1, waiting for transfers between devices, shards(): attention = lax.psum(matmul(attended, output_full), 'tensor')  70.9 us
    psum x1, waiting for transfers between devices, shards(): lax.psum((shared_part + routed_sum).astype(jnp.bfloat16), 'tensor')  66.1 us
    all_to_all x1, waiting for transfers between devices, shards(): lax.all_to_all(grad_input_rows, 'expert', split_axis=0, concat_axis=0, ti...  52.9 us
    reduce_scatter x1, waiting for transfers between devices, shards(): lax.psum_scatter(query_grad.astype(jnp.bfloat16), 'expert', scatter_dimen...  47.5 us
  transfers between devices with their start and end apart: 22, of which 16 were waited for; matrix products, arithmetic and copies ran while one was open for 26% of the time, Pallas kernels for 0%

commit v1 on v0

v1 whole, which is shorter than its diff:
```python
import math

import jax
import jax.numpy as jnp
from jax import lax
from jax.experimental import pallas as pl
from jax.experimental.pallas import tpu as pltpu
from jax.sharding import PartitionSpec as P

D = 2048
HEAD_DIM = 128
ROPE_DIM = 64
KV_RANK = 512
TOP = 6


EPSILON = 1e-06
ROUTE_SCALE = 2.446
ROPE_BASE = 50000.0
MASKED = -1e30


def matmul(left, right):
    return jnp.dot(left, right, preferred_element_type=jnp.float32)


def matmul_nt(left, right):
    return lax.dot_general(
        left, right, (((1,), (1,)), ((), ())), preferred_element_type=jnp.float32
    )


def matmul_tn(left, right):
    return lax.dot_general(
        left, right, (((0,), (0,)), ((), ())), preferred_element_type=jnp.float32
    )


def rotary_tables(length):
    position = jnp.arange(length).astype(jnp.float32)
    exponent = jnp.arange(ROPE_DIM // 2).astype(jnp.float32) * (2.0 / ROPE_DIM)
    angles = position[:, None] * jnp.exp(-math.log(ROPE_BASE) * exponent)[None, :]
    return (jnp.cos(angles), jnp.sin(angles))


def rotate(values, cosine, sine):
    half = values.shape[-1] // 2
    first = values[..., :half]
    second = values[..., half:]
    return jnp.concatenate(
        [first * cosine - second * sine, second * cosine + first * sine], axis=-1
    )


def sigmoid(values):
    return 1.0 / (1.0 + jnp.exp(-values))


def norm_backward(grad_normed, values, inverse, gain):
    gain_grad = jnp.sum(grad_normed * values * inverse, axis=0)
    scaled = grad_normed * gain
    inner = jnp.mean(scaled * values, axis=1, keepdims=True)
    return (inverse * scaled - values * inverse * inverse * inverse * inner, gain_grad)


MESH = pl.DeviceIdType.MESH
ANY = pl.BlockSpec(memory_space=pl.ANY)
VMEM = pl.BlockSpec(memory_space=pltpu.VMEM)


def xor_bit(value, bit):
    return value + bit - 2 * bit * lax.rem(value // bit, 2)


def add_rows(dst, first, second, rows):
    step = math.gcd(rows, 16)

    def body(i, carry):
        at = pl.ds(pl.multiple_of(i * step, step), step)
        total = first[at].astype(jnp.float32) + second[at].astype(jnp.float32)
        dst[at] = total.astype(dst.dtype)
        return carry

    lax.fori_loop(0, rows // step, body, 0)


class Fabric:
    def __init__(self, send, recv, local):
        self.send, self.recv, self.local = send, recv, local
        self.used = self.local_used = 0
        self.e = lax.axis_index("expert")
        self.z = lax.axis_index("tensor")
        self.partner = (xor_bit(self.e, 1), self.z)
        self.xn = (xor_bit(self.e, 2), self.z)
        self.yn = (xor_bit(self.e, 4), self.z)
        self.line = (self.e, xor_bit(self.z, 1))
        self.middle = (self.e, 3 - self.z)
        self.inner = jnp.logical_or(self.z == 1, self.z == 2)

    def copy(self, src, dst, device):
        k = self.used
        self.used += 1
        return pltpu.make_async_remote_copy(
            src_ref=src,
            dst_ref=dst,
            send_sem=self.send.at[k],
            recv_sem=self.recv.at[k],
            device_id=device,
            device_id_type=MESH,
        )

    def here(self, src, dst):
        k = self.local_used
        self.local_used += 1
        return pltpu.make_async_copy(src, dst, self.local.at[k])

    def slot(self, bits):
        e = self.e
        for bit in (1, 2, 4):
            if bits & bit:
                e = xor_bit(e, bit)
        return e


class Gather:
    sends, locals = 9, 2

    def __init__(self, array, axis=0, at=0.0, early=False):
        self.array, self.axis, self.at, self.early = array, axis, at, early
        r, c = array.shape
        shape = (r, 8 * c) if axis else (8, r, c)
        self.arrays, self.outs = [array], [jax.ShapeDtypeStruct(shape, array.dtype)]
        self.in_spec = self.out_spec = ANY
        self.scratch = [pltpu.VMEM(array.shape, array.dtype)]
        self.span = self.load = 3 * 2 * array.size * array.dtype.itemsize / 160e3

    def finish(self):
        return self.at + self.wait + self.load + 5.0

    def plain(self):
        return [lax.all_gather(self.array, "expert", axis=self.axis, tiled=bool(self.axis))]

    def steps(self, fab, src, dst, held):
        r, c = self.array.shape
        h = (r // 2 + 15) // 16 * 16 if r > 16 else r // 2
        parts = {0: pl.ds(0, h), 1: pl.ds(h, r - h), None: pl.ds(0, r)}

        def view(bits, part=None):
            slot = fab.slot(bits)
            if self.axis:
                return dst.at[parts[part], pl.ds(pl.multiple_of(slot * c, c), c)]
            return dst.at[slot, parts[part]]

        def forward(bits, device, part=None):
            return fab.copy(view(bits, part), view(bits, part), device)

        load, store = fab.here(src, held), fab.here(held, view(0))
        to_x, to_y, to_p = (fab.copy(src, view(0), d) for d in (fab.xn, fab.yn, fab.partner))
        lo, hi = forward(2, fab.yn, 0), forward(4, fab.xn, 1)
        px, py = forward(2, fab.partner), forward(4, fab.partner)
        plo, phi = forward(6, fab.partner, 0), forward(6, fab.partner, 1)

        def begin():
            for each in (to_x, to_y, to_p, load):
                each.start()

        def keep():
            load.wait()
            store.start()

        def from_x():
            to_x.wait_recv()
            lo.start()
            px.start()

        def from_y():
            to_y.wait_recv()
            hi.start()
            py.start()

        def corner_lo():
            lo.wait_recv()
            plo.start()

        def corner_hi():
            hi.wait_recv()
            phi.start()

        def arrive():
            store.wait()
            for each in (to_p, px, py, plo, phi):
                each.wait_recv()

        def end():
            for each in (to_x, to_y, to_p, lo, hi, px, py, plo, phi):
                each.wait_send()

        t, s, w = self.at, self.span, self.wait
        return [
            (self.start, begin),
            (self.start + 2, keep),
            (t + w + 2 + s * 2 / 3, from_x),
            (t + w + 2 + s * 2 / 3, from_y),
            (t + w + 3 + s, corner_lo),
            (t + w + 3 + s, corner_hi),
            (self.finish() if self.early else 1e8, arrive),
            (1e9, end),
        ]


class Swap:
    sends, locals = 7, 2

    def __init__(self, array, at=0.0):
        self.array, self.at = array, at
        self.arrays, self.outs = [array], [jax.ShapeDtypeStruct(array.shape, array.dtype)]
        self.in_spec = self.out_spec = ANY
        self.scratch = [pltpu.VMEM(array.shape[1:], array.dtype)]
        self.load = array.size * array.dtype.itemsize / 80e3

    def plain(self):
        return [lax.all_to_all(self.array, "expert", split_axis=0, concat_axis=0, tiled=True)]

    def steps(self, fab, src, dst, held):
        e = fab.e
        load, store = fab.here(src.at[e], held), fab.here(held, dst.at[e])
        copies = []
        for bits in (6, 7, 2, 3, 4, 5, 1):
            other = fab.slot(bits)
            copies.append(fab.copy(src.at[other], dst.at[e], (other, fab.z)))

        def begin():
            for each in copies:
                each.start()
            load.start()

        def keep():
            load.wait()
            store.start()

        def end():
            store.wait()
            for each in copies:
                each.wait()

        return [(self.start, begin), (self.start + 2, keep), (1e9, end)]


class Scatter:
    def __init__(self, array, axis=0, pieces=1, at=0.0, out_dtype=None, source=None):
        self.array, self.axis, self.pieces, self.at, self.source = array, axis, pieces, at, source
        if axis:
            r, c = array.shape[0], array.shape[1] // 8
        else:
            r, c = array.shape[1:]
        self.r, self.c = r, c
        self.arrays, self.outs = [array], [jax.ShapeDtypeStruct((r, c), out_dtype or array.dtype)]
        if source:
            self.arrays = []
        self.in_spec, self.out_spec = ANY, VMEM
        d = array.dtype
        self.scratch = [
            pltpu.VMEM((4, r, c), d),
            pltpu.VMEM((4, r, c), d),
            pltpu.VMEM((2, r, c), d),
            pltpu.VMEM((r, c), d),
            pltpu.VMEM((r, c), d),
        ]
        self.sends, self.locals = 10 * pieces, 4 * pieces
        self.load = 3 * 2 * r * c * d.itemsize / 160e3
        self.span = self.load / pieces

    def plain(self):
        if self.axis:
            out = lax.psum_scatter(self.array, "expert", scatter_dimension=1, tiled=True)
        else:
            out = lax.psum_scatter(self.array, "expert", scatter_dimension=0, tiled=False)
        return [out.astype(self.outs[0].dtype)]

    def steps(self, fab, *refs):
        src, out, theirs, mine, near, turn, last = refs if self.source is None else (self.source(), *refs)
        r, c = self.r, self.c
        rows = r // self.pieces
        half = rows // 2
        order = (6, 2, 4, 0)
        place = {0: 0, 2: 1, 4: 2, 6: 3}
        result = []

        def block(bits, at):
            slot = fab.slot(bits)
            if self.axis:
                return src.at[at, pl.ds(pl.multiple_of(slot * c, c), c)]
            return src.at[slot, at]

        for k in range(self.pieces):
            both = pl.ds(k * rows, rows)
            a, b = pl.ds(k * rows, half), pl.ds(k * rows + half, half)
            give = [fab.copy(block(s ^ 1, both), theirs.at[place[s], both], fab.partner) for s in order]
            load = [fab.here(block(s, both), mine.at[place[s], both]) for s in order]
            a0 = fab.copy(mine.at[3, a], near.at[1, a], fab.xn)
            a1 = fab.copy(mine.at[1, a], near.at[0, a], fab.xn)
            b0 = fab.copy(mine.at[3, b], near.at[1, b], fab.yn)
            b1 = fab.copy(mine.at[2, b], near.at[0, b], fab.yn)
            ta = fab.copy(turn.at[a], last.at[a], fab.yn)
            tb = fab.copy(turn.at[b], last.at[b], fab.xn)

            def begin(give=give, load=load):
                for g, h in zip(give, load, strict=True):
                    g.start()
                    h.start()

            def chip(k=k, give=give, load=load, both=both, a0=a0, a1=a1, b0=b0, b1=b1):
                for i, s in enumerate(order):
                    give[i].wait_recv()
                    load[i].wait()
                    q = place[s]
                    add_rows(mine.at[q, both], mine.at[q, both], theirs.at[q, both], rows)
                    if s == 6:
                        a0.start()
                        b0.start()
                    elif s == 2:
                        a1.start()
                    elif s == 4:
                        b1.start()

            def turn_a(a=a, a0=a0, ta=ta):
                a0.wait_recv()
                add_rows(turn.at[a], mine.at[2, a], near.at[1, a], half)
                ta.start()

            def turn_b(b=b, b0=b0, tb=tb):
                b0.wait_recv()
                add_rows(turn.at[b], mine.at[1, b], near.at[1, b], half)
                tb.start()

            def own(a=a, b=b, a1=a1, b1=b1, both=both):
                a1.wait_recv()
                b1.wait_recv()
                a1.wait_send()
                b1.wait_send()

            def close(a=a, b=b, give=give, a0=a0, b0=b0, ta=ta, tb=tb, both=both):
                ta.wait()
                tb.wait()
                step = math.gcd(rows, 16)

                def body(i, carry):
                    at = pl.ds(pl.multiple_of(i * step + both.start, step), step)
                    total = mine[0, at].astype(jnp.float32) + near[0, at].astype(jnp.float32)
                    out[at] = (total + last[at].astype(jnp.float32)).astype(out.dtype)
                    return carry

                lax.fori_loop(0, rows // step, body, 0)
                a0.wait_send()
                b0.wait_send()
                for g in give:
                    g.wait_send()

            t, s, w = self.at, self.span, self.wait
            result += [
                (t + k * 1e-3, begin),
                (t + 3 + w * 0.9 + k * s, chip),
                (t + w + 6 + (k + 0.7) * s, turn_a),
                (t + w + 6 + (k + 0.7) * s, turn_b),
                (t + w + 7 + (k + 0.9) * s, own),
                (t + w + 9 + (k + 1.3) * s, close),
            ]
        return result


class Line:
    def __init__(self, array, pieces=8, at=0.0, early=False):
        self.array, self.pieces, self.at, self.early = array, pieces, at, early
        self.arrays, self.outs = [array], [jax.ShapeDtypeStruct(array.shape, array.dtype)]
        self.in_spec = self.out_spec = VMEM
        self.scratch = [pltpu.VMEM(array.shape, array.dtype)] * 3
        self.sends, self.locals = 3 * pieces, 0
        self.load = 2 * array.size * array.dtype.itemsize / 80e3
        self.span = self.load / pieces

    def finish(self):
        return self.at + self.wait + self.load + 8.0

    def plain(self):
        return [lax.psum(self.array, "tensor")]

    def steps(self, fab, src, out, mixed, from_end, from_mid):
        inner = fab.inner
        rows = self.array.shape[0] // self.pieces
        result = []
        for k in range(self.pieces):
            at = pl.ds(k * rows, rows)
            up = fab.copy(src.at[at], from_end.at[at], fab.line)
            across = fab.copy(mixed.at[at], from_mid.at[at], fab.middle)
            down = fab.copy(out.at[at], out.at[at], fab.line)

            def begin(up=up):
                @pl.when(jnp.logical_not(inner))
                def _():
                    up.start()

            def meet(at=at, up=up, across=across):
                @pl.when(inner)
                def _():
                    up.wait_recv()
                    add_rows(mixed.at[at], src.at[at], from_end.at[at], rows)
                    across.start()

            def answer(at=at, across=across, down=down):
                @pl.when(inner)
                def _():
                    across.wait_recv()
                    add_rows(out.at[at], mixed.at[at], from_mid.at[at], rows)
                    down.start()

            def arrive(down=down):
                @pl.when(jnp.logical_not(inner))
                def _():
                    down.wait_recv()

            def end(up=up, across=across, down=down):
                @pl.when(inner)
                def _():
                    across.wait_send()
                    down.wait_send()

                @pl.when(jnp.logical_not(inner))
                def _():
                    up.wait_send()

            t, s, w = self.at, self.span, self.wait
            result += [
                (t, begin),
                (t + w + 2 + (k + 1) * s, meet),
                (t + w + 4 + (k + 2) * s, answer),
                (self.finish() if self.early else 1e8, arrive),
                (1e9, end),
            ]
        return result


def exchange(tasks, cid, fast):
    if not fast:
        return [out for task in tasks for out in task.plain()]
    lined = any(isinstance(task, (Line, Attend)) for task in tasks)
    planar = any(task.sends and not isinstance(task, (Line, Attend)) for task in tasks)
    swaps = any(isinstance(task, Swap) for task in tasks)
    busy = {True: 0.0, False: 0.0}
    for task in sorted(tasks, key=lambda each: each.at):
        task.wait = busy[isinstance(task, (Line, Attend))]
        if getattr(task, "source", None):
            task.wait = max(0.0, task.wait - task.at)
        busy[isinstance(task, (Line, Attend))] += task.load
    queue = [task for task in sorted(tasks, key=lambda each: each.at) if isinstance(task, (Gather, Swap))]
    for i, task in enumerate(queue):
        task.start = task.at
        if i > 1 and any(getattr(each, "early", False) for each in queue):
            task.start = max(task.at, queue[i - 2].at + queue[i - 2].wait + 2.1 + queue[i - 2].load * 2 / 3)
    given = sum(len(task.arrays) for task in tasks)
    made = sum(len(task.outs) for task in tasks)

    def kernel(*refs):
        ins, outs = list(refs[:given]), list(refs[given : given + made])
        send, recv, local = refs[-3:]
        scratch = list(refs[given + made : -3])
        fab = Fabric(send, recv, local)
        barrier = pltpu.get_barrier_semaphore()
        devices = []
        if swaps:
            devices = [(fab.slot(bits), fab.z) for bits in range(1, 8)]
        elif planar:
            devices = [fab.partner, fab.xn, fab.yn]
        if lined:
            devices.append(fab.line)
        for device in devices:
            pl.semaphore_signal(barrier, inc=1, device_id=device, device_id_type=MESH)
        if lined:

            @pl.when(fab.inner)
            def _():
                pl.semaphore_signal(barrier, inc=1, device_id=fab.middle, device_id_type=MESH)
                pl.semaphore_wait(barrier, len(devices) + 1)

            @pl.when(jnp.logical_not(fab.inner))
            def _():
                pl.semaphore_wait(barrier, len(devices))

        else:
            pl.semaphore_wait(barrier, len(devices))
        steps = []
        for task in tasks:
            own = [ins.pop(0) for _ in task.arrays]
            own += [outs.pop(0) for _ in task.outs]
            own += [scratch.pop(0) for _ in task.scratch]
            task.refs = own
        for task in tasks:
            steps += task.steps(fab, *task.refs)
        for _, step in sorted(steps, key=lambda pair: pair[0]):
            step()

    return pl.pallas_call(
        kernel,
        out_shape=[out for task in tasks for out in task.outs],
        in_specs=[spec for task in tasks for spec in (getattr(task, "in_specs", None) or [task.in_spec] * len(task.arrays))],
        out_specs=[task.out_spec for task in tasks for _ in task.outs],
        scratch_shapes=[s for task in tasks for s in task.scratch]
        + [
            pltpu.SemaphoreType.DMA((sum(task.sends for task in tasks),)),
            pltpu.SemaphoreType.DMA((sum(task.sends for task in tasks),)),
            pltpu.SemaphoreType.DMA((max(1, sum(task.locals for task in tasks)),)),
        ],
        compiler_params=pltpu.CompilerParams(collective_id=cid, has_side_effects=True, vmem_limit_bytes=63 * 1024 * 1024),
        name=f"exchange_{cid}",
    )(*[array for task in tasks for array in task.arrays])


def dot_nt(left, right):
    return lax.dot_general(left, right, (((1,), (1,)), ((), ())), preferred_element_type=jnp.float32)


def add_block(dst, first, second, rows):
    def body(i, carry):
        at = pl.ds(pl.multiple_of(i * 16, 16), 16)
        dst[at] = (first[at].astype(jnp.float32) + second[at].astype(jnp.float32)).astype(dst.dtype)
        return carry

    lax.fori_loop(0, rows // 16, body, 0)


def expert_stage(rows, mixing, upstream, gate, up, down, common_gate, common_up, common_down, cid):
    length, width = rows.shape
    pair = 2 * length
    units, common = gate.shape[1], common_gate.shape[1]
    segment, shared = lanes(units), lanes(common)
    wide = 2 * segment
    total = wide + shared
    both = 2 * total
    tile = 256
    low = rows.dtype
    half = width // 2
    full = width + 128
    cuts = (pl.ds(0, half), pl.ds(half, full - half))

    def kernel(
        x_h, mix_h, dy_h, wg_h, wu_h, wd_h, sg_h, su_h, sd_h,
        out_h, all_h, hm_h, dgu_h, own, own_mix,
        xs, mixs, dys, wg, wu, ws, wd, wc, dh, dgu, gs, us, ost, grads, theirs, near, turn, last,
        send, recv, local,
    ):
        fab = Fabric(send, recv, local)
        e = fab.e
        core = lax.rem(e, 2)
        mine = pl.ds(pl.multiple_of(core * length, length), length)
        other = pl.ds(pl.multiple_of((1 - core) * length, length), length)
        pairs = [fab.slot(bits) // 2 for bits in (0, 2, 4, 6)]

        barrier = pltpu.get_barrier_semaphore()
        for device in (fab.partner, fab.xn, fab.yn):
            pl.semaphore_signal(barrier, inc=1, device_id=device, device_id_type=MESH)
        pl.semaphore_wait(barrier, 3)

        quarter = length // 2

        def view(ref, bits, part=None):
            slot = fab.slot(bits)
            base = lax.rem(slot, 2) * length
            if part is None:
                return ref.at[slot // 2, pl.ds(pl.multiple_of(base, length), length)]
            return ref.at[slot // 2, pl.ds(pl.multiple_of(base + part * quarter, quarter), quarter)]

        def spread(src, ref):
            def forward(bits, device, part=None):
                return fab.copy(view(ref, bits, part), view(ref, bits, part), device)

            return {
                "load": fab.here(src, view(ref, 0)),
                "x": fab.copy(src, view(ref, 0), fab.xn),
                "y": fab.copy(src, view(ref, 0), fab.yn),
                "p": fab.copy(src, view(ref, 0), fab.partner),
                "lo": forward(2, fab.yn, 0),
                "hi": forward(4, fab.xn, 1),
                "px": forward(2, fab.partner),
                "py": forward(4, fab.partner),
                "plo": forward(6, fab.partner, 0),
                "phi": forward(6, fab.partner, 1),
            }

        moves = [spread(mix_h, mixs), spread(x_h, xs)]
        for name in ("x", "y", "p", "load"):
            for move in moves:
                move[name].start()
        def experts_of(src, dst):
            return [fab.here(src.at[i], dst.at[pl.ds(i * segment, units)]) for i in range(2)]

        def blocks_of(src, dst, first):
            d = src.shape[2]
            return [fab.here(src.at[j], dst.at[pl.ds(first, common), pl.ds(j * d, d)]) for j in range(src.shape[0])]

        load_out = experts_of(wd_h, wd) + blocks_of(sd_h, wc, 0)
        load_dy = [fab.here(dy_h.at[p], dys.at[p]) for p in pairs]
        load_in = experts_of(wg_h, wg) + experts_of(wu_h, wu) + blocks_of(sg_h, ws, 0) + blocks_of(su_h, ws, shared)
        for load in (*load_out, *load_dy, *load_in):
            load.start()
        for ref in (wd, wg, wu):
            for first in (units, segment + units):
                ref[first : first + segment - units, :] = jnp.zeros((segment - units, width), low)
        for ref, first in ((wc, common), (ws, common), (ws, shared + common)):
            ref[first : first + shared - common, :] = jnp.zeros((shared - common, width), low)
        keep = [fab.here(xs.at[p], all_h.at[p]) for p in pairs]
        keep_hm = [fab.here(dh.at[p], hm_h.at[p]) for p in pairs]
        keep_dgu = [fab.here(dgu, dgu_h.at[p]) for p in pairs]
        keep_out = [fab.here(ost.at[k % 2], out_h.at[p]) for k, p in enumerate(pairs)]

        give = [[fab.copy(grads.at[k, other, cut], theirs.at[k, :, cut], fab.partner) for cut in cuts] for k in range(4)]
        a, b = cuts
        a0 = fab.copy(grads.at[3, mine, a], near.at[1, :, a], fab.xn)
        a1 = fab.copy(grads.at[1, mine, a], near.at[0, :, a], fab.xn)
        b0 = fab.copy(grads.at[3, mine, b], near.at[1, :, b], fab.yn)
        b1 = fab.copy(grads.at[2, mine, b], near.at[0, :, b], fab.yn)
        ta = fab.copy(turn.at[:, a], last.at[:, a], fab.yn)
        tb = fab.copy(turn.at[:, b], last.at[:, b], fab.xn)

        def at_tile(n, first=0):
            return pl.ds(pl.multiple_of(first + n * tile, tile), tile)

        def back(p):
            def one(n, carry):
                at = at_tile(n)
                dh[p, :, at] = dot_nt(dys[p], wd[at, :]).astype(low)
                return carry

            lax.fori_loop(0, wide // tile, one, 0)
            dh[p, :, wide:total] = dot_nt(dys[p], wc[...]).astype(low)

        def hidden(p, k):
            def one(n, carry):
                at = at_tile(n)
                gs[:, at] = dot_nt(xs[p], wg[at, :])
                us[:, at] = dot_nt(xs[p], wu[at, :])
                return carry

            lax.fori_loop(0, wide // tile, one, 0)
            together = dot_nt(xs[p], ws[...])
            gs[:, wide:total] = together[:, :shared]
            us[:, wide:total] = together[:, shared:]

        def middle(p, k):
            step = 32

            def some(i, carry):
                at = pl.ds(pl.multiple_of(i * step, step), step)
                lane = lax.broadcasted_iota(jnp.int32, (step, 128), 1)
                expert = lax.rem(lane, 64)
                mixed = mixs[p, at].astype(jnp.float32)
                first = jnp.sum(jnp.where(expert == 2 * e, mixed, 0.0), axis=1, keepdims=True)
                second = jnp.sum(jnp.where(expert == 2 * e + 1, mixed, 0.0), axis=1, keepdims=True)

                def part(lo, hi, weight, to_gate, to_up):
                    gate, up = gs[at, lo:hi], us[at, lo:hi]
                    grad = dh[p, at, lo:hi].astype(jnp.float32)
                    logistic = sigmoid(gate)
                    active = gate * logistic
                    value = active * up
                    share = jnp.sum(value * grad, axis=1, keepdims=True)
                    grad = grad * weight
                    dh[p, at, lo:hi] = (value * weight).astype(low)
                    dgu[at, to_gate : to_gate + hi - lo] = (grad * up * (logistic + active * (1.0 - logistic))).astype(low)
                    dgu[at, to_up : to_up + hi - lo] = (grad * active).astype(low)
                    return share

                one = part(0, segment, first, 0, wide)
                two = part(segment, wide, second, segment, wide + segment)
                part(wide, total, 1.0, 2 * wide, 2 * wide + shared)
                shares = jnp.where(lane == 2 * e, one, jnp.where(lane == 2 * e + 1, two, 0.0))
                grads[k, at, width:full] = shares.astype(low)
                return carry

            lax.fori_loop(0, pair // step, some, 0)

        def inputs(p, k, first, count):
            def one(n, carry):
                at = at_tile(n, first)
                value = matmul(dgu[:, :wide], wg[:, at]) + matmul(dgu[:, wide : 2 * wide], wu[:, at])
                grads[k, :, at] = (value + matmul(dgu[:, 2 * wide :], ws[:, at])).astype(low)
                return carry

            lax.fori_loop(0, count // tile, one, 0)

        def outputs(p, k):
            if k > 1:
                keep_out[k - 2].wait()

            def one(n, carry):
                at = at_tile(n)
                value = matmul(dh[p, :, :wide], wd[:, at]) + matmul(dh[p, :, wide:], wc[:, at])
                ost[k % 2, :, at] = value.astype(low)
                return carry

            lax.fori_loop(0, width // tile, one, 0)
            keep_out[k].start()

        def compute(k):
            p = pairs[k]
            keep[k].start()
            hidden(p, k)
            if k > 0:
                keep_dgu[k - 1].wait()
            middle(p, k)
            keep_dgu[k].start()
            keep_hm[k].start()
            inputs(p, k, 0, half)
            give[k][0].start()
            inputs(p, k, half, half)
            give[k][1].start()

        def chip(k, part):
            give[k][part].wait_recv()
            cut = cuts[part]
            add_block(grads.at[k, mine, cut], grads.at[k, mine, cut], theirs.at[k, :, cut], length)

        for load in load_out:
            load.wait()
        for k in range(4):
            load_dy[k].wait()
            back(pairs[k])
        for load in load_in:
            load.wait()
        for move in moves:
            move["load"].wait()
            move["p"].wait_recv()
        compute(0)
        for move in moves:
            move["x"].wait_recv()
            move["lo"].start()
            move["px"].start()
        for move in moves:
            move["y"].wait_recv()
            move["hi"].start()
            move["py"].start()
        chip(0, 0)
        chip(0, 1)
        for move in moves:
            move["px"].wait_recv()
        compute(1)
        for move in moves:
            move["lo"].wait_recv()
            move["plo"].start()
            move["hi"].wait_recv()
            move["phi"].start()
        chip(1, 0)
        a1.start()
        chip(1, 1)
        for move in moves:
            move["py"].wait_recv()
        compute(2)
        chip(2, 1)
        b1.start()
        chip(2, 0)
        for move in moves:
            move["plo"].wait_recv()
            move["phi"].wait_recv()
        compute(3)
        chip(3, 0)
        a0.start()
        chip(3, 1)
        b0.start()
        outputs(pairs[0], 0)
        outputs(pairs[1], 1)
        outputs(pairs[2], 2)
        a0.wait_recv()
        add_block(turn.at[:, a], grads.at[2, mine, a], near.at[1, :, a], length)
        ta.start()
        b0.wait_recv()
        add_block(turn.at[:, b], grads.at[1, mine, b], near.at[1, :, b], length)
        tb.start()
        outputs(pairs[3], 3)
        a1.wait_recv()
        b1.wait_recv()
        ta.wait_recv()
        tb.wait_recv()

        def sum_up(i, carry):
            at = pl.ds(pl.multiple_of(i * 16, 16), 16)
            here = pl.ds(pl.multiple_of(core * length + i * 16, 16), 16)
            value = grads[0, here].astype(jnp.float32) + near[0, at].astype(jnp.float32)
            value = (value + last[at].astype(jnp.float32)).astype(low)
            own[at] = value[:, :width]
            own_mix[at] = value[:, width:]
            return carry

        lax.fori_loop(0, length // 16, sum_up, 0)
        for move in moves:
            for name in ("x", "y", "p", "lo", "hi", "px", "py", "plo", "phi"):
                move[name].wait_send()
        for k in range(4):
            for each in give[k]:
                each.wait_send()
            keep[k].wait()
            keep_hm[k].wait()
        keep_dgu[3].wait()
        keep_out[2].wait()
        keep_out[3].wait()
        for each in (a0, a1, b0, b1, ta, tb):
            each.wait_send()

    shape = jax.ShapeDtypeStruct
    vmem = pltpu.VMEM
    return pl.pallas_call(
        kernel,
        out_shape=[
            shape((4, pair, width), low),
            shape((4, pair, width), low),
            shape((4, pair, total), low),
            shape((4, pair, both), low),
            shape((length, width), low),
            shape((length, 128), low),
        ],
        in_specs=[ANY] * 9,
        out_specs=[ANY] * 4 + [VMEM] * 2,
        scratch_shapes=[
            vmem((4, pair, width), low),
            vmem((4, pair, 128), low),
            vmem((4, pair, width), low),
            vmem((wide, width), low),
            vmem((wide, width), low),
            vmem((2 * shared, width), low),
            vmem((wide, width), low),
            vmem((shared, width), low),
            vmem((4, pair, total), low),
            vmem((pair, both), low),
            vmem((pair, total), jnp.float32),
            vmem((pair, total), jnp.float32),
            vmem((2, pair, width), low),
            vmem((4, pair, full), low),
            vmem((4, length, full), low),
            vmem((2, length, full), low),
            vmem((length, full), low),
            vmem((length, full), low),
            pltpu.SemaphoreType.DMA((32,)),
            pltpu.SemaphoreType.DMA((32,)),
            pltpu.SemaphoreType.DMA((56,)),
        ],
        compiler_params=pltpu.CompilerParams(
            collective_id=cid, has_side_effects=True, vmem_limit_bytes=63 * 1024 * 1024
        ),
        name="expert_stage",
    )(rows, mixing, upstream.reshape(4, pair, width), gate, up, down, common_gate, common_up, common_down)


class Weights:
    sends, locals, load = 0, 80, 0.0

    def __init__(self, rows, grads, hidden, upstream, experts, units, common, own, at=0.0, pace=2.0):
        self.arrays = [rows, grads, hidden, upstream]
        self.in_spec = self.out_spec = ANY
        self.at, self.pace = at, pace
        self.tokens, self.width = rows.shape
        self.total = hidden.shape[1]
        self.experts, self.units, self.common, self.own = experts, units, common, own
        self.pad = lanes(units)
        self.wide = experts * self.pad
        self.shared = self.total - self.wide
        low = rows.dtype
        shape = jax.ShapeDtypeStruct
        whole, part = shape((experts, units, self.width), low), shape((self.width // own, common, own), low)
        self.outs = [whole, whole, whole, part, part, part]
        tile = pltpu.VMEM((2, experts, units, own), low)
        piece = pltpu.VMEM((2, common, own), low)
        self.scratch = [
            pltpu.VMEM(rows.shape, low),
            pltpu.VMEM(upstream.shape, low),
            pltpu.VMEM(hidden.shape, low),
            pltpu.VMEM(hidden.shape, low),
            pltpu.VMEM((self.total, self.tokens), low),
            pltpu.VMEM((2 * self.total, self.tokens), low),
            tile,
            tile,
            tile,
            piece,
            piece,
            piece,
        ]

    def plain(self):
        rows, grads, hidden, upstream = self.arrays
        low, wide, shared = rows.dtype, self.wide, self.shared
        into, out = matmul_tn(grads, rows).astype(low), matmul_tn(hidden, upstream).astype(low)

        def pick(array, first):
            return jnp.stack([array[first + i * self.pad :][: self.units] for i in range(self.experts)])

        def blocks(array, first):
            return array[first : first + self.common].reshape(self.common, -1, self.own).transpose(1, 0, 2)

        return [
            pick(into, 0),
            pick(into, wide),
            pick(out, 0),
            blocks(into, 2 * wide),
            blocks(into, 2 * wide + shared),
            blocks(out, wide),
        ]

    def steps(
        self, fab, x_h, g_h, h_h, y_h, gate_o, up_o, down_o, cg_o, cu_o, cd_o,
        xs, ys, s0, s1, ht, gt, gst, ust, dst, cgs, cus, cds,
    ):
        units, pad, wide, total, own, common = self.units, self.pad, self.wide, self.total, self.own, self.common
        columns = self.width // own
        load_h, load_y, load_x = fab.here(h_h, s0), fab.here(y_h, ys), fab.here(x_h, xs)
        load_lo = fab.here(g_h.at[:, pl.ds(0, total)], s1)
        load_hi = fab.here(g_h.at[:, pl.ds(total, total)], s0)

        def puts(n, whole, part):
            cols = pl.ds(n * own, own)
            copies = [fab.here(s.at[n % 2, i], o.at[i, :, cols]) for s, o in whole for i in range(self.experts)]
            return copies + [fab.here(s.at[n % 2], o.at[n]) for s, o in part]

        put_in = [puts(n, ((gst, gate_o), (ust, up_o)), ((cgs, cg_o), (cus, cu_o))) for n in range(columns)]
        put_out = [puts(n, ((dst, down_o),), ((cds, cd_o),)) for n in range(columns)]

        def begin():
            for each in (load_h, load_y, load_lo, load_x):
                each.start()

        def turn(dst_ref, src_ref, first):
            for at in range(0, total, 128):
                dst_ref[first + at : first + at + 128, :] = src_ref[:, at : at + 128].T

        def turn_hidden():
            load_h.wait()
            turn(ht, s0, 0)
            load_hi.start()

        def turn_lo():
            load_lo.wait()
            turn(gt, s1, 0)

        def turn_hi():
            load_hi.wait()
            turn(gt, s0, total)

        def store(stage, n, value):
            for i in range(self.experts):
                stage[n % 2, i] = value[i * pad : i * pad + units].astype(stage.dtype)

        def down(n):
            def step():
                if n == 0:
                    load_y.wait()
                if n >= 2:
                    for each in put_out[n - 2]:
                        each.wait()
                value = matmul(ht[...], ys[:, n * own : (n + 1) * own])
                store(dst, n, value)
                cds[n % 2] = value[wide : wide + common].astype(cds.dtype)
                for each in put_out[n]:
                    each.start()

            return step

        def gate(n):
            def step():
                if n == 0:
                    load_x.wait()
                if n >= 2:
                    for each in put_in[n - 2]:
                        each.wait()
                store(gst, n, matmul(gt[:wide], xs[:, n * own : (n + 1) * own]))

            return step

        def up(n):
            def step():
                value = matmul(gt[wide:], xs[:, n * own : (n + 1) * own])
                store(ust, n, value)
                cgs[n % 2] = value[wide : wide + common].astype(cgs.dtype)
                cus[n % 2] = value[wide + self.shared : wide + self.shared + common].astype(cus.dtype)
                for each in put_in[n]:
                    each.start()

            return step

        def end():
            for each in (*put_out[-2], *put_out[-1], *put_in[-2], *put_in[-1]):
                each.wait()

        t, p = self.at, self.pace
        result = [(t, begin), (t + 3, turn_hidden)]
        t += 4
        for n in range(columns):
            result.append((t, down(n)))
            t += 0.7 * p
        result.append((t, turn_lo))
        t += 0.7 * p
        result.append((t, turn_hi))
        t += 0.7 * p
        for n in range(columns):
            result.append((t, gate(n)))
            t += 0.6 * p
            result.append((t, up(n)))
            t += 0.8 * p
        result.append((1e9, end))
        return result


class Attend:
    names = ("sum", "normed", "query_nope", "query_rope", "latent_raw", "compressed", "key_rope", "expanded", "weights", "attended")

    def __init__(self, hidden, pre_gain, latent_gain, cosine, sine, segments, query, latent, expand, output, at=0.0):
        length = hidden.shape[0]
        self.heads = query.shape[1] // (HEAD_DIM + ROPE_DIM)
        self.at = at
        low = hidden.dtype
        shape = jax.ShapeDtypeStruct
        self.arrays = [
            hidden, pre_gain[None], latent_gain[None], cosine, sine, segments[:, None], segments[None],
            query, latent, expand, output,
        ]
        self.in_specs = [VMEM] * 7 + [ANY] * 4
        self.out_spec = VMEM
        heads = self.heads
        self.line = Line(shape(hidden.shape, low), at=at)
        self.outs = [
            shape(hidden.shape, low),
            shape(hidden.shape, low),
            shape((length, heads * HEAD_DIM), low),
            shape((length, heads * ROPE_DIM), low),
            shape((length, KV_RANK), jnp.float32),
            shape((length, KV_RANK), low),
            shape((length, ROPE_DIM), low),
            shape((length, heads * 2 * HEAD_DIM), low),
            shape((heads, length, length), jnp.float32),
            shape((length, heads * HEAD_DIM), low),
        ]
        self.scratch = [pltpu.VMEM(w.shape, low) for w in (query, latent, expand, output)]
        self.scratch += [pltpu.VMEM((length, query.shape[1]), jnp.float32), pltpu.VMEM(hidden.shape, low)] + self.line.scratch
        self.sends, self.locals, self.load = self.line.sends, 4, self.line.load

    def steps(
        self, fab, x, pre_gain, latent_gain, cos, sin, seg_col, seg_row, q_h, l_h, e_h, o_h,
        out, normed, q_nope, q_rope, raw, compressed, k_rope, expanded, probs, attended,
        wq, wl, we, wo, qs, part, mixed, from_end, from_mid,
    ):
        length = x.shape[0]
        loads = [fab.here(a, b) for a, b in ((l_h, wl), (q_h, wq), (e_h, we), (o_h, wo))]
        low = jnp.bfloat16
        scale = 1.0 / math.sqrt(HEAD_DIM + ROPE_DIM)

        def begin():
            for each in loads:
                each.start()

        def norm():
            def some(i, carry):
                at = pl.ds(pl.multiple_of(i * 32, 32), 32)
                v = x[at].astype(jnp.float32)
                inverse = lax.rsqrt(jnp.mean(v * v, axis=1, keepdims=True) + EPSILON)
                normed[at] = (v * inverse * pre_gain[...]).astype(low)
                return carry

            lax.fori_loop(0, length // 32, some, 0)

        def latent():
            loads[0].wait()
            every = dot_nt(normed[...], wl[...])
            value = every[:, :KV_RANK]
            raw[...] = value
            inverse = lax.rsqrt(jnp.mean(value * value, axis=1, keepdims=True) + EPSILON)
            compressed[...] = (value * inverse * latent_gain[...]).astype(low)
            k_rope[...] = rotate(every[:, KV_RANK:], cos[...], sin[...]).astype(low)

        def queries():
            loads[1].wait()

            def one(n, carry):
                at = pl.ds(pl.multiple_of(n * 256, 256), 256)
                qs[:, at] = matmul(normed[...], wq[:, at])
                return carry

            lax.fori_loop(0, qs.shape[1] // 256, one, 0)
            for h in range(self.heads):
                first = h * (HEAD_DIM + ROPE_DIM)
                q_nope[:, h * HEAD_DIM : (h + 1) * HEAD_DIM] = qs[:, first : first + HEAD_DIM].astype(low)
                turned = rotate(qs[:, first + HEAD_DIM : first + HEAD_DIM + ROPE_DIM], cos[...], sin[...])
                q_rope[:, h * ROPE_DIM : (h + 1) * ROPE_DIM] = turned.astype(low)

        def expand():
            loads[2].wait()
            for n in range(0, expanded.shape[1], 256):
                expanded[:, n : n + 256] = matmul(compressed[...], we[:, n : n + 256]).astype(low)

        def head(h):
            def step():
                first = 2 * HEAD_DIM * h
                scores = dot_nt(q_nope[:, h * HEAD_DIM : (h + 1) * HEAD_DIM], expanded[:, first : first + HEAD_DIM])
                scores = scores + dot_nt(q_rope[:, h * ROPE_DIM : (h + 1) * ROPE_DIM], k_rope[...])
                row = lax.broadcasted_iota(jnp.int32, (length, length), 0)
                column = lax.broadcasted_iota(jnp.int32, (length, length), 1)
                allowed = jnp.logical_and(column <= row, seg_col[...] == seg_row[...])
                scores = jnp.where(allowed, scores * scale, MASKED)
                raised = jnp.exp(scores - jnp.max(scores, axis=1, keepdims=True))
                chance = raised / jnp.sum(raised, axis=1, keepdims=True)
                probs[h] = chance
                value = matmul(chance.astype(low), expanded[:, first + HEAD_DIM : first + 2 * HEAD_DIM])
                attended[:, h * HEAD_DIM : (h + 1) * HEAD_DIM] = value.astype(low)

            return step

        def project():
            loads[3].wait()

            def one(n, carry):
                at = pl.ds(pl.multiple_of(n * 256, 256), 256)
                part[:, at] = matmul(attended[...], wo[:, at]).astype(low)
                return carry

            lax.fori_loop(0, part.shape[1] // 256, one, 0)

        t = self.at
        result = [(t, begin), (t + 0.1, norm), (t + 1, latent), (t + 3, queries), (t + 6, expand)]
        result += [(t + 7 + h, head(h)) for h in range(self.heads)]
        result.append((t + 12, project))
        self.line.at, self.line.wait = t + 14, 0.0
        return result + self.line.steps(fab, part, out, mixed, from_end, from_mid)


class Tail:
    sends, load = 0, 0.0

    def __init__(self, latent_line, normed_line, raw, latent_gain, normed, latent, hidden, pre_gain, grad_middle, small, at=0.0):
        self.at = at
        self.latent_line, self.normed_line = latent_line, normed_line
        self.arrays = [raw, latent_gain[None], normed, latent, hidden, pre_gain[None], grad_middle, small]
        self.in_spec = self.out_spec = VMEM
        low = hidden.dtype
        length, width = hidden.shape
        self.outs = [jax.ShapeDtypeStruct(hidden.shape, low)]
        depth = lanes(latent.shape[0])
        self.scratch = [
            pltpu.VMEM((length, depth), low),
            pltpu.VMEM((depth, length), low),
            pltpu.VMEM((latent.shape[0], width), low),
            pltpu.VMEM(small.shape, jnp.float32),
            pltpu.VMEM((length, width), jnp.float32),
            pltpu.VMEM((1, width), jnp.float32),
        ]
        self.locals = 1

    def latent_source(self):
        return self.refs[11]

    def small_source(self):
        return self.refs[12]

    def steps(self, fab, raw, latent_gain, normed, latent, hidden, pre_gain, grad_middle, small, out, gl, turned, lg, sm, gn, pre):
        latent_sum, normed_sum = self.latent_line.refs[1], self.normed_line.refs[1]
        length, width = hidden.shape
        rank = raw.shape[1]
        low = gl.dtype
        tile = 256

        def latent_back():
            grad, value = latent_sum[:, :rank].astype(jnp.float32), raw[...]
            inverse = lax.rsqrt(jnp.mean(value * value, axis=1, keepdims=True) + EPSILON)
            gain_grad = jnp.sum(grad * value * inverse, axis=0, keepdims=True)
            scaled = grad * latent_gain[...]
            inner = jnp.mean(scaled * value, axis=1, keepdims=True)
            gl[:, :rank] = (inverse * scaled - value * (inverse * inverse * inverse * inner)).astype(low)
            gl[:, rank:] = latent_sum[:, rank:]
            sm[...] = small[...]
            part = rank // 8
            for j in range(8):
                sm[j, 2:3, :part] = gain_grad[:, j * part : (j + 1) * part]
            for n in range(0, gl.shape[1], 128):
                turned[n : n + 128, :] = gl[:, n : n + 128].T

            def one(n, carry):
                at = pl.ds(pl.multiple_of(n * tile, tile), tile)
                lg[:, at] = matmul(turned[: lg.shape[0], :], normed[:, at]).astype(low)
                return carry

            lax.fori_loop(0, width // tile, one, 0)

        def normed_back():
            def one(n, carry):
                at = pl.ds(pl.multiple_of(n * tile, tile), tile)
                gn[:, at] = normed_sum[:, at].astype(jnp.float32) + matmul(gl[:, : latent.shape[0]], latent[:, at])
                return carry

            lax.fori_loop(0, width // tile, one, 0)
            pre[...] = jnp.zeros_like(pre)

            def some(i, carry):
                at = pl.ds(pl.multiple_of(i * 16, 16), 16)
                value, grad = hidden[at].astype(jnp.float32), gn[at]
                inverse = lax.rsqrt(jnp.mean(value * value, axis=1, keepdims=True) + EPSILON)
                pre[...] += jnp.sum(grad * value * inverse, axis=0, keepdims=True)
                scaled = grad * pre_gain[...]
                inner = jnp.mean(scaled * value, axis=1, keepdims=True)
                back = inverse * scaled - value * (inverse * inverse * inverse * inner)
                out[at] = (grad_middle[at] + back).astype(low)
                return carry

            lax.fori_loop(0, length // 16, some, 0)
            part = width // 8
            for j in range(8):
                sm[j, 0:1, :] = pre[:, j * part : (j + 1) * part]

        return [
            (self.latent_line.finish() + 0.1, latent_back),
            (self.normed_line.finish() + 0.1, normed_back),
        ]


def lanes(width):
    return -(-width // 128) * 128


def pad_to(array, axis, size):
    widths = [(0, 0)] * array.ndim
    widths[axis] = (0, size - array.shape[axis])
    return jnp.pad(array, widths) if widths[axis][1] else array


def shards(
    hidden_in,
    segment_ids,
    expert_ids,
    query_weight,
    latent_weight,
    expand_weight,
    output_weight,
    prenorm,
    latentnorm,
    postnorm,
    router_weight,
    shared_gate,
    shared_up,
    shared_down,
    expert_gate,
    expert_up,
    expert_down,
    cotangent,
):
    groups = lax.axis_size("expert")
    ranks = lax.axis_size("tensor")
    fast = groups == 8 and ranks == 4
    me = lax.axis_index("expert")
    local_experts, _, units = expert_gate.shape
    experts = local_experts * groups
    length = hidden_in.shape[0]
    tokens = groups * length
    own_d = prenorm.shape[0]
    own_latent = latentnorm.shape[0]
    common = shared_gate.shape[1] // groups
    unit_pad, common_pad = lanes(units), lanes(common)
    low = jnp.bfloat16

    small = jnp.concatenate(
        [
            prenorm[None],
            postnorm[None],
            pad_to(latentnorm[None], 1, own_d),
            jnp.zeros((5, own_d), low),
            router_weight.T,
        ],
        axis=0,
    )
    small_full, latent_full, query_full, expand_full, output_full = exchange(
        [
            Gather(small, at=0.0),
            Gather(latent_weight.T, axis=1, at=0.1),
            Gather(query_weight, at=0.2),
            Gather(expand_weight, at=0.3),
            Gather(output_weight, axis=1, at=0.4),
        ],
        0,
        fast,
    )
    query_full = query_full.reshape(D, -1)
    expand_full = expand_full.reshape(KV_RANK, -1)
    pre_gain = small_full[:, 0].reshape(D).astype(jnp.float32)
    post_gain = small_full[:, 1].reshape(D).astype(jnp.float32)
    latent_gain = small_full[:, 2, :own_latent].reshape(KV_RANK).astype(jnp.float32)
    router_full = small_full[:, 8:].transpose(1, 0, 2).reshape(experts, D)

    heads = query_full.shape[1] // (HEAD_DIM + ROPE_DIM)
    hidden = hidden_in.astype(jnp.float32)
    cosine, sine = rotary_tables(length)
    inverse_pre = lax.rsqrt(jnp.mean(hidden * hidden, axis=1, keepdims=True) + EPSILON)
    scale = 1.0 / math.sqrt(HEAD_DIM + ROPE_DIM)
    segments = segment_ids[0]

    def unit_blocks(weight):
        return weight.reshape(groups, common, own_d)

    beside = [
        Gather(cotangent, at=0.1),
        Swap(unit_blocks(shared_gate.T), at=0.2),
        Swap(unit_blocks(shared_up.T), at=0.3),
        Swap(unit_blocks(shared_down), at=0.4),
    ]
    if fast:
        attend = Attend(
            hidden_in, pre_gain, latent_gain, cosine, sine, segments, query_full, latent_full, expand_full, output_full,
            at=0.5,
        )
        (
            upstream_all,
            common_gate,
            common_up,
            common_down,
            attention,
            normed,
            query_nope,
            query_rope,
            latent_raw,
            compressed,
            key_rope,
            expanded,
            probabilities,
            attended,
        ) = exchange([*beside, attend], 1, fast)
    else:
        normed = (hidden * inverse_pre * pre_gain).astype(low)
        query_raw = matmul(normed, query_full).reshape(length, heads, HEAD_DIM + ROPE_DIM)
        query_nope = query_raw[:, :, :HEAD_DIM].astype(low)
        query_rope = rotate(query_raw[:, :, HEAD_DIM:], cosine[:, None, :], sine[:, None, :]).astype(low)
        latent_all = matmul_nt(normed, latent_full)
        latent_raw = latent_all[:, :KV_RANK]
        norm_latent = lax.rsqrt(jnp.mean(latent_raw * latent_raw, axis=1, keepdims=True) + EPSILON)
        compressed = (latent_raw * norm_latent * latent_gain).astype(low)
        key_rope = rotate(latent_all[:, KV_RANK:], cosine, sine).astype(low)
        expanded = matmul(compressed, expand_full).astype(low)
        parts = expanded.reshape(length, heads, 2 * HEAD_DIM)
        position = jnp.arange(length)
        allowed = (position[None, :] <= position[:, None]) & (segments[:, None] == segments[None, :])
        raw = jnp.einsum("qhd,khd->hqk", query_nope, parts[:, :, :HEAD_DIM], preferred_element_type=jnp.float32)
        raw = raw + jnp.einsum("qhr,kr->hqk", query_rope, key_rope, preferred_element_type=jnp.float32)
        scores = jnp.where(allowed[None], raw * scale, MASKED)
        raised = jnp.exp(scores - jnp.max(scores, axis=2, keepdims=True))
        probabilities = raised / jnp.sum(raised, axis=2, keepdims=True)
        attended = (
            jnp.einsum(
                "hqk,khd->qhd", probabilities.astype(low), parts[:, :, HEAD_DIM:], preferred_element_type=jnp.float32
            )
            .astype(low)
            .reshape(length, heads * HEAD_DIM)
        )
        upstream_all, common_gate, common_up, common_down, attention = exchange(
            [*beside, Line(matmul(attended, output_full).astype(low))], 1, fast
        )
    query_nope = query_nope.reshape(length, heads, HEAD_DIM)
    query_rope = query_rope.reshape(length, heads, ROPE_DIM)
    key_nope = expanded.reshape(length, heads, 2 * HEAD_DIM)[:, :, :HEAD_DIM]
    values = expanded.reshape(length, heads, 2 * HEAD_DIM)[:, :, HEAD_DIM:]
    probabilities_low = probabilities.astype(low)
    inverse_latent = lax.rsqrt(jnp.mean(latent_raw * latent_raw, axis=1, keepdims=True) + EPSILON)
    middle = hidden + attention.astype(jnp.float32)
    inverse_post = lax.rsqrt(jnp.mean(middle * middle, axis=1, keepdims=True) + EPSILON)
    normed_mid = (middle * inverse_post * post_gain).astype(low)
    affinity = sigmoid(matmul_nt(normed_mid, router_full))
    chosen = jnp.any(
        expert_ids[:, :, None] == jnp.arange(experts, dtype=jnp.int32)[None, None, :], axis=1
    ).astype(jnp.float32)
    selected = chosen * affinity
    selected_total = jnp.sum(selected, axis=1, keepdims=True)
    mixing = ROUTE_SCALE * selected / selected_total

    upstream_rows = upstream_all.reshape(tokens, D)
    gate_rows, up_rows = expert_gate.transpose(0, 2, 1), expert_up.transpose(0, 2, 1)
    wide = local_experts * unit_pad
    total = wide + common_pad
    if fast:
        high = mixing.astype(low)
        rest = (mixing - high.astype(jnp.float32)).astype(low)
        pair = jnp.concatenate([pad_to(high, 1, 64), pad_to(rest, 1, 64)], axis=1)
        mixture_rows, token_rows, mixed_hidden, grad_both, grad_own, mixing_grad_own = expert_stage(
            normed_mid,
            pair,
            upstream_all,
            gate_rows,
            up_rows,
            expert_down,
            common_gate,
            common_up,
            common_down,
            2,
        )
        token_rows = token_rows.reshape(tokens, D)
        mixed_hidden = mixed_hidden.reshape(tokens, total)
        grad_both = grad_both.reshape(tokens, 2 * total)
    else:
        token_rows = lax.all_gather(normed_mid, "expert", axis=0, tiled=True)
        mixing_own = lax.dynamic_slice_in_dim(
            lax.all_gather(mixing, "expert", axis=0, tiled=True), me * local_experts, local_experts, axis=1
        )
        segment = jnp.minimum(jnp.arange(total) // unit_pad, local_experts)
        scales = jnp.concatenate([mixing_own, jnp.ones((tokens, 1), jnp.float32)], axis=1)
        mixing_wide = sum(
            jnp.where(segment[None, :] == i, scales[:, i : i + 1], 0.0) for i in range(local_experts + 1)
        )

        def padded(weight):
            return jnp.concatenate([pad_to(weight[i], 0, unit_pad) for i in range(local_experts)], axis=0)

        def joined(blocks):
            return pad_to(blocks.transpose(1, 0, 2).reshape(common, D), 0, common_pad)

        weight_in = jnp.concatenate([padded(gate_rows), padded(up_rows), joined(common_gate), joined(common_up)], axis=0)
        weight_out = jnp.concatenate([padded(expert_down), joined(common_down)], axis=0)
        every = matmul_nt(token_rows, weight_in)
        gate = jnp.concatenate([every[:, :wide], every[:, 2 * wide : 2 * wide + common_pad]], axis=1)
        up = jnp.concatenate([every[:, wide : 2 * wide], every[:, 2 * wide + common_pad :]], axis=1)
        logistic = sigmoid(gate)
        unit_hidden = gate * logistic * up
        mixed_hidden = (unit_hidden * mixing_wide).astype(low)
        mixture_rows = matmul(mixed_hidden, weight_out).astype(low)
        grad_unit = matmul_nt(upstream_rows, weight_out)
        mixing_share = unit_hidden * grad_unit
        mixing_grad = jnp.stack(
            [jnp.sum(mixing_share[:, i * unit_pad : (i + 1) * unit_pad], axis=1) for i in range(local_experts)], axis=1
        )
        grad_hidden = grad_unit * mixing_wide
        grad_up = (grad_hidden * gate * logistic).astype(low)
        grad_gate = (grad_hidden * up * logistic * (1.0 + gate * (1.0 - logistic))).astype(low)
        grad_both = jnp.concatenate(
            [grad_gate[:, :wide], grad_up[:, :wide], grad_gate[:, wide:], grad_up[:, wide:]], axis=1
        )
        spread = jnp.arange(lanes(experts))
        mixing_grad_wide = sum(
            jnp.where(spread[None, :] == me * local_experts + i, mixing_grad[:, i : i + 1], 0.0)
            for i in range(local_experts)
        ).astype(low)
        grad_own = lax.psum_scatter(matmul(grad_both, weight_in).astype(low), "expert", tiled=True)
        mixing_grad_own = lax.psum_scatter(mixing_grad_wide, "expert", tiled=True)
    (
        grad_mid,
        grad_mixing,
        mixture_own,
        expert_gate_grad,
        expert_up_grad,
        expert_down_grad,
        common_gate_grad,
        common_up_grad,
        common_down_grad,
    ) = exchange(
        [
            Line(grad_own),
            Line(mixing_grad_own, pieces=1, at=-0.1),
            Scatter(mixture_rows.reshape(groups, length, D), pieces=4, at=0.2),
            Weights(
                token_rows, grad_both, mixed_hidden, upstream_rows, local_experts, units, common, own_d, at=1.0
            ),
        ],
        4,
        fast,
    )
    grad_mid = grad_mid.astype(jnp.float32)
    grad_mixing = grad_mixing[:, :experts].astype(jnp.float32)
    grad_selected = (
        ROUTE_SCALE
        * chosen
        * (
            grad_mixing / selected_total
            - jnp.sum(grad_mixing * selected, axis=1, keepdims=True) / (selected_total * selected_total)
        )
    )
    grad_logits = (grad_selected * affinity * (1.0 - affinity)).astype(low)
    router_grad = matmul_tn(grad_logits, normed_mid)
    grad_mid = grad_mid + matmul(grad_logits, router_full)
    upstream = cotangent.astype(jnp.float32)
    grad_middle_norm, post_grad = norm_backward(grad_mid, middle, inverse_post, post_gain)
    grad_middle = upstream + grad_middle_norm
    grad_attention = grad_middle.astype(low)
    output_grad = matmul_tn(attended, grad_attention)
    grad_attended = matmul_nt(grad_attention, output_full).astype(low).reshape(length, heads, HEAD_DIM)
    grad_probs = jnp.einsum("qhd,khd->hqk", grad_attended, values, preferred_element_type=jnp.float32)
    inner = jnp.sum(probabilities * grad_probs, axis=2, keepdims=True)
    grad_scores = (probabilities * (grad_probs - inner)).astype(low)
    grad_query_nope = scale * jnp.einsum("hqk,khd->qhd", grad_scores, key_nope, preferred_element_type=jnp.float32)
    grad_query_rope = scale * jnp.einsum("hqk,kr->qhr", grad_scores, key_rope, preferred_element_type=jnp.float32)
    grad_key_nope = scale * jnp.einsum("hqk,qhd->khd", grad_scores, query_nope, preferred_element_type=jnp.float32)
    grad_key_rope = scale * jnp.einsum("hqk,qhr->kr", grad_scores, query_rope, preferred_element_type=jnp.float32)
    grad_values = jnp.einsum("hqk,qhd->khd", probabilities_low, grad_attended, preferred_element_type=jnp.float32)
    grad_query = (
        jnp.concatenate(
            [grad_query_nope, rotate(grad_query_rope, cosine[:, None, :], -sine[:, None, :])], axis=2
        )
        .astype(low)
        .reshape(length, heads * (HEAD_DIM + ROPE_DIM))
    )
    query_grad = matmul_tn(normed, grad_query)
    grad_expanded = (
        jnp.concatenate([grad_key_nope, grad_values], axis=2).astype(low).reshape(length, heads * 2 * HEAD_DIM)
    )
    expand_grad = matmul_tn(compressed, grad_expanded)
    grad_key = pad_to(rotate(grad_key_rope, cosine, -sine), 1, lanes(ROPE_DIM))
    grad_latent_terms = jnp.concatenate([matmul_nt(grad_expanded, expand_full), grad_key], axis=1).astype(low)
    small_grad = jnp.concatenate(
        [
            jnp.zeros((groups, 1, own_d), jnp.float32),
            post_grad.reshape(groups, 1, own_d),
            jnp.zeros((groups, 14, own_d), jnp.float32),
            router_grad.reshape(experts, groups, own_d).transpose(1, 0, 2),
        ],
        axis=1,
    )
    latent_line = Line(grad_latent_terms, at=0.0, early=True)
    normed_line = Line(matmul_nt(grad_query, query_full).astype(low), at=0.05, early=True)
    dense = [
        Scatter(query_grad.astype(low).reshape(groups, own_d, -1), pieces=2, at=0.2),
        Scatter(expand_grad.astype(low).reshape(groups, own_latent, -1), at=0.4),
        Scatter(output_grad.astype(low), axis=1, pieces=2, at=0.6),
    ]
    swaps = [
        Swap(common_gate_grad, at=30.0),
        Swap(common_up_grad, at=30.1),
        Swap(common_down_grad, at=30.2),
    ]
    if fast:
        tail = Tail(
            latent_line, normed_line, latent_raw, latent_gain, normed, latent_full, hidden_in, pre_gain, grad_middle,
            small_grad,
        )
        shape = jax.ShapeDtypeStruct
        (
            _,
            _,
            query_out,
            expand_out,
            output_out,
            common_gate_out,
            common_up_out,
            common_down_out,
            mixture,
            latent_out,
            small_out,
            input_gradient,
        ) = exchange(
            [
                latent_line,
                normed_line,
                *dense,
                *swaps,
                Line(mixture_own, at=0.1),
                Scatter(shape((latent_full.shape[0], D), low), axis=1, pieces=2, at=24.0, source=tail.latent_source),
                Scatter(shape(small_grad.shape, jnp.float32), at=52.0, source=tail.small_source),
                tail,
            ],
            5,
            fast,
        )
    else:
        grad_latent_sum, grad_normed_sum, query_out, expand_out, output_out = exchange(
            [latent_line, normed_line, *dense], 5, fast
        )
        grad_latent_sum = grad_latent_sum.astype(jnp.float32)
        grad_latent_raw, latent_norm_grad = norm_backward(
            grad_latent_sum[:, :KV_RANK], latent_raw, inverse_latent, latent_gain
        )
        grad_latent = jnp.concatenate(
            [grad_latent_raw, grad_latent_sum[:, KV_RANK : KV_RANK + ROPE_DIM]], axis=1
        ).astype(low)
        latent_grad = matmul_tn(grad_latent, normed)
        grad_normed = grad_normed_sum.astype(jnp.float32) + matmul(grad_latent, latent_full)
        grad_hidden_in, pre_grad = norm_backward(grad_normed, hidden, inverse_pre, pre_gain)
        input_gradient = (grad_middle + grad_hidden_in).astype(low)
        small_grad = small_grad.at[:, 0].set(pre_grad.reshape(groups, own_d))
        small_grad = small_grad.at[:, 2, :own_latent].set(latent_norm_grad.reshape(groups, own_latent))
        mixture, latent_out, small_out, common_gate_out, common_up_out, common_down_out = exchange(
            [
                Line(mixture_own),
                Scatter(latent_grad.astype(low), axis=1, pieces=2, at=0.2),
                Scatter(small_grad, at=0.1),
                *swaps,
            ],
            6,
            fast,
        )
    block_output = (middle + mixture.astype(jnp.float32)).astype(low)

    def unit_rows(back):
        return back.reshape(groups * common, own_d).astype(jnp.float32)

    return (
        block_output,
        input_gradient,
        query_out.astype(jnp.float32),
        latent_out.T.astype(jnp.float32),
        expand_out.astype(jnp.float32),
        output_out.astype(jnp.float32),
        small_out[0],
        small_out[2, :own_latent],
        small_out[1],
        small_out[16:].T,
        unit_rows(common_gate_out).T,
        unit_rows(common_up_out).T,
        unit_rows(common_down_out),
        expert_gate_grad.astype(jnp.float32).transpose(0, 2, 1),
        expert_up_grad.astype(jnp.float32).transpose(0, 2, 1),
        expert_down_grad.astype(jnp.float32),
    )


def solution(mesh):
    placed = (
        P("expert", None),
        P("expert", None),
        P("expert", None),
        P("expert", "tensor"),
        P("expert", None),
        P("expert", "tensor"),
        P("tensor", "expert"),
        P("expert"),
        P("expert"),
        P("expert"),
        P("expert", None),
        P("expert", "tensor"),
        P("expert", "tensor"),
        P("tensor", "expert"),
        P("expert", None, "tensor"),
        P("expert", None, "tensor"),
        P("expert", "tensor", None),
        P("expert", None),
    )
    return jax.shard_map(
        shards,
        mesh=mesh,
        in_specs=placed,
        out_specs=(
            P("expert", None),
            P("expert", None),
            P("expert", "tensor"),
            P("expert", None),
            P("expert", "tensor"),
            P("tensor", "expert"),
            P("expert"),
            P("expert"),
            P("expert"),
            P("expert", None),
            P("expert", "tensor"),
            P("expert", "tensor"),
            P("tensor", "expert"),
            P("expert", None, "tensor"),
            P("expert", None, "tensor"),
            P("expert", "tensor", None),
        ),
        check_vma=False,
    )
```

time: 1390 us -> 451 us (0.32)
  waiting for transfers between devices: 739 us -> 0 us
  Pallas kernels: 0 us -> 372 us
  blocking collectives: 193 us -> 0 us
  matrix products: 179 us -> 16.4 us
  local copies, waits for them, and re-layouts: 154 us -> 20.6 us
  other arithmetic: 82 us -> 32.5 us
  starting transfers between devices: 23.1 us -> 0 us
  between operations: 17.7 us -> 1.44 us
    pallas_call x0 -> x5, Pallas kernels: none -> 372 us  [the longest x4 267 us: exchange(): pl.pallas_call(kernel, out_shape=[out for task in tasks for out in task.o...]
    all_to_all x4 -> x0, waiting for transfers between devices: 265 us -> none  [the longest x1 127 us: shards(): lax.all_to_all(grad_outgoing, 'expert', split_axis=0, concat_axis=0, tile...]
    reduce_scatter x8 -> x0, waiting for transfers between devices: 174 us -> none  [the longest x1 47.5 us: shards(): lax.psum_scatter(query_grad.astype(jnp.bfloat16), 'expert', scatter_dimen...]
    all_gather x7 -> x0, waiting for transfers between devices: 159 us -> none  [the longest x1 87.5 us: shards(): lax.all_gather(shared_gate, 'expert', axis=0, tiled=True)]
    psum x3 -> x0, waiting for transfers between devices: 137 us -> none  [the longest x1 70.9 us: shards(): attention = lax.psum(matmul(attended, output_full), 'tensor')]
    all_gather x3 -> x0, blocking collectives: 135 us -> none  [the longest x1 117 us: shards(): lax.all_gather(router_weight, 'expert', axis=0, tiled=True)]
    dot_general x13 -> x1, matrix products: 104 us -> 0.23 us  [shards(): jnp.einsum('hqk,qhd->khd', probabilities_low, grad_attended, preferred_el...]
    convert_element_type x4 -> x1, local copies, waits for them, and re-layouts: 39.9 us -> 0.66 us  [shards(): small_full[:, 2, :own_latent].reshape(KV_RANK).astype(jnp.float32)]
  transfers between devices with their start and end apart: 22 -> 0, of which waited for: 16 -> 0; matrix products, arithmetic and copies ran while one was open for 26% -> 0% of each run, Pallas kernels for 0% -> 0%
where the time goes in v1:
time: 451 us; the launch traced here: 443 us
  Pallas kernels  372 us (82%)
  other arithmetic  32.5 us (7%)
  local copies, waits for them, and re-layouts  20.6 us (5%)
  matrix products  16.4 us (4%)
    pallas_call x4, Pallas kernels, exchange(): pl.pallas_call(kernel, out_shape=[out for task in tasks for out in task.o...  267 us
    pallas_call x1, Pallas kernels, expert_stage(): pl.pallas_call(kernel, out_shape=[shape((4, pair, width), low), shape((4,...  105 us

profile of v1, /device:TPU:0, one launch (start us, length us, event | category | flops | bytes accessed | tf_op | source)
XLA Modules:
  0.0 443.5 jit_solution(14666461235360186863)
XLA Ops:
  1.8 0.7 broadcast_in_dim.12
  2.4 0.7 pad.16
  3.1 0.7 broadcast_in_dim.13
  3.8 0.7 fusion.23
  4.5 1.9 concatenate.23.refs_0_
  6.6 1.5 copy.86.refs_9_
  8.1 1.2 fusion.28
  9.3 0.7 copy.107
  10.0 0.7 copy.106
  10.7 48.5 %exchange_0.1 = (bf16[8,24,256]{2,1,0:T(8,128)(2,1)}, bf16[576,2048]{1,0:T(8,128)(2,1)}, bf16[8,256,768]{2,1,0:T(8,128)(2,1)}, bf16[8,64,1024]{2,1,0:T(8,128)(2,1)}, bf16[512,2048]{1,0:T(8,128)(2,1)}) custom-call(bf16[24,256]{1,0:T(8,128)(2,1)} %concatenate.23.refs_0_, bf16[576,256]{1,0:T(8,128)(2,1)} %bitcast.135, bf16[256,768]{1,0:T(8,128)(2,1)} %refs_2_.1, ...), custom_call_target="tpu_custom_call" | custom-call | tf_op jit(solution)/shard_map/exchange_0/pallas_call | solution.py:501
  59.2 0.7 convert_reduce_fusion
  59.9 0.7 reshape.256.refs_6_.refs_10_
  60.6 0.8 slice_convert_fusion
  61.4 0.9 slice_bitcast_fusion
  62.9 65.1 %exchange_1.1 = (bf16[8,256,2048]{2,1,0:T(8,128)(2,1)}, bf16[8,88,256]{2,1,0:T(8,128)(2,1)}, bf16[8,88,256]{2,1,0:T(8,128)(2,1)}, bf16[8,88,256]{2,1,0:T(8,128)(...) custom-call(bf16[256,2048]{1,0:T(8,128)(2,1)} %refs_0_.1, ...), custom_call_target="tpu_custom_call" | custom-call | tf_op jit(solution)/shard_map/exchange_1/pallas_call | solution.py:501
  128.1 1.9 copy.113
  129.9 2.1 multiply_reduce_fusion.2
  132.1 0.8 copy.102
  133.2 1.0 fusion.30
  134.7 1.0 copy-done.6
  136.3 0.7 fusion.24.mix_h
  137.0 105.1 %expert_stage.1 = (bf16[4,512,2048]{2,1,0:T(8,128)(2,1)}, bf16[4,512,2048]{2,1,0:T(8,128)(2,1)}, bf16[4,512,896]{2,1,0:T(8,128)(2,1)}, bf16[4,512,1792]{2,1,0:T(...) custom-call(bf16[256,2048]{1,0:T(8,128)(2,1)} %copy-done.6, bf16[256,128]{1,0:T(8,128)(2,1)} %fusion.24.mix_h, ...), custom_call_target="tpu_custom_call" | custom-call | tf_op jit(solution)/shard_map/expert_stage/pallas_call | solution.py:808
  242.1 64.7 %exchange_4.1 = (bf16[256,2048]{1,0:T(8,128)(2,1)}, bf16[256,128]{1,0:T(8,128)(2,1)}, bf16[256,2048]{1,0:T(8,128)(2,1)}, bf16[2,352,2048]{2,1,0:T(8,128)(2,1)}, ...) custom-call(bf16[256,2048]{1,0:T(8,128)(2,1)} %get-tuple-element.72., ...), custom_call_target="tpu_custom_call" | custom-call | tf_op jit(solution)/shard_map/exchange_4/pallas_call | solution.py:501
  306.9 1.1 fusion.17
  308.0 1.0 fusion.21
  309.0 1.5 fusion.32
  310.5 2.3 multiply_reduce_fusion
  312.9 1.0 subtract_add_fusion.refs_15_
  314.5 1.5 convolution_convert_fusion.5
  316.0 1.1 copy.124
  317.1 1.5 pad_maximum_fusion.1.refs_16_
  322.2 2.0 convolution_convert_fusion.2.refs_1_
  324.7 0.8 pad_maximum_fusion.refs_0_
  325.5 1.5 convolution_convert_fusion.3
  327.0 2.1 convolution_convert_fusion.1.refs_4_
  329.0 2.7 convolution_convert_fusion
  331.7 89.0 %exchange_5.1 = (bf16[256,640]{1,0:T(8,128)(2,1)}, bf16[256,2048]{1,0:T(8,128)(2,1)}, bf16[256,768]{1,0:T(8,128)(2,1)}, bf16[64,1024]{1,0:T(8,128)(2,1)}, bf16[5...) custom-call(bf16[256,640]{1,0:T(8,128)(2,1)} %pad_maximum_fusion.ref, ...), custom_call_target="tpu_custom_call" | custom-call | tf_op jit(solution)/shard_map/exchange_5/pallas_call | solution.py:501
  420.8 3.5 add_convert_fusion
  426.0 0.7 convert_element_type.252
  426.7 0.8 convert_element_type.253
  427.5 0.9 convert_bitcast_fusion.4
  428.4 0.9 bitcast_convert_fusion
  429.3 0.9 convert_element_type.249
  430.3 1.3 convert_bitcast_fusion.2
  431.5 3.7 convert_element_type.258
  435.2 1.1 copy-done.14
  436.3 5.9 %convert_bitcast_fusion = (f32[2,2048,352]{1,2,0:T(8,128)}, f32[2,2048,352]{1,2,0:T(8,128)}) fusion(bf16[2,352,2048]{2,1,0:T(8,128)(2,1)S(1)} %copy-done.14, bf16[2,352,2048]{2,1,0:T(8,128)(2,1)S(1)} %copy-done.13), kind=kLoop, calls=%fused_computation | loop fusion | flops 2883584 | bytes 17301504 | tf_op jit(solution)/shard_map/transpose | solution.py:1602
  442.2 1.0 copy.139
  (115 shorter events, 9.8 us)
Async XLA Ops:
  0.7 59.3 %copy-start.38 = (f32[32]{0:T(128)}, f32[32]{0:T(128)S(1)}, u32[]{:S(2)}) copy-start(f32[32]{0:T(128)S(1)} %multiply_exponential_fusion) | copy-start | bytes 388
  9.3 53.6 %copy-start.15 = (f32[256,32]{1,0:T(8,128)}, f32[256,32]{1,0:T(8,128)S(1)}, u32[]{:S(2)}) copy-start(f32[256,32]{1,0:T(8,128)S(1)} %get-tuple-element.120.refs_7_) | copy-start | bytes 98308
  62.3 72.4 %copy-start.34 = (bf16[8,2,8,256]{3,2,0,1:T(8,128)(2,1)}, bf16[8,2,8,256]{3,2,0,1:T(8,128)(2,1)S(1)}, u32[]{:S(2)}) copy-start(bf16[8,2,8,256]{3,2,0,1:T(8,128)(2,1)S(1)} %copy.126) | copy-start | bytes 196612
  128.0 4.0 copy-start.33
  128.1 4.8 %copy-start.20 = (bf16[256,1024]{1,0:T(8,128)(2,1)S(1)}, bf16[256,1024]{1,0:T(8,128)(2,1)}, u32[]{:S(2)}) copy-start(bf16[256,1024]{1,0:T(8,128)(2,1)} %get-tuple-element.80) | copy-start | bytes 1572868
  129.9 4.2 copy-start
  129.9 4.2 copy-start.3
  134.7 1.0 copy-start.6
  242.1 68.4 %copy-start.35 = (bf16[8,2,8,256]{3,2,0,1:T(8,128)(2,1)S(1)}, bf16[8,2,8,256]{3,2,0,1:T(8,128)(2,1)}, u32[]{:S(2)}) copy-start(bf16[8,2,8,256]{3,2,0,1:T(8,128)(2,1)} %copy-done.34) | copy-start | bytes 196612
  306.9 3.6 copy-start.1
  306.9 3.6 copy-start.4
  310.5 2.3 copy-start.9
  312.9 1.6 copy-start.8
  314.5 12.5 %copy-start.2 = (f32[256,2048]{1,0:T(8,128)}, f32[256,2048]{1,0:T(8,128)S(1)}, u32[]{:S(2)}) copy-start(f32[256,2048]{1,0:T(8,128)S(1)} %subtract_add_fusion.refs_15_) | copy-start | bytes 6291460
  314.5 2.6 copy-start.40
  314.5 4.1 copy-start.5
  317.1 1.8 copy-start.17
  318.8 1.0 copy-start.19
  319.3 0.9 copy-start.21
  319.3 1.3 copy-start.39
  319.3 2.0 copy-start.18
  319.8 1.7 copy-start.36
  319.8 2.0 copy-start.30
  319.8 2.0 copy-start.31
  320.2 1.9 copy-start.11
  322.2 2.1 copy-start.10
  324.2 1.3 copy-start.28
  324.2 2.7 copy-start.27
  327.0 2.1 copy-start.7
  420.8 3.5 copy-start.37
  420.8 5.2 %copy-start.32 = (bf16[64,1024]{1,0:T(8,128)(2,1)S(1)}, bf16[64,1024]{1,0:T(8,128)(2,1)}, u32[]{:S(2)}) copy-start(bf16[64,1024]{1,0:T(8,128)(2,1)} %get-tuple-element.95) | copy-start | bytes 393220
  420.8 5.9 %copy-start.29 = (bf16[512,256]{1,0:T(8,128)(2,1)S(1)}, bf16[512,256]{1,0:T(8,128)(2,1)}, u32[]{:S(2)}) copy-start(bf16[512,256]{1,0:T(8,128)(2,1)} %get-tuple-element.96) | copy-start | bytes 786436
  420.8 6.7 %copy-start.26 = (bf16[576,256]{1,0:T(8,128)(2,1)S(1)}, bf16[576,256]{1,0:T(8,128)(2,1)}, u32[]{:S(2)}) copy-start(bf16[576,256]{1,0:T(8,128)(2,1)} %get-tuple-element.94) | copy-start | bytes 884740
  424.3 4.1 copy-start.23
  424.3 5.0 %copy-start.22 = (bf16[256,768]{1,0:T(8,128)(2,1)S(1)}, bf16[256,768]{1,0:T(8,128)(2,1)}, u32[]{:S(2)}) copy-start(bf16[256,768]{1,0:T(8,128)(2,1)} %get-tuple-element.93) | copy-start | bytes 1179652
  426.0 4.3 copy-start.24
  426.0 4.3 copy-start.25
  428.4 3.1 copy-start.12
  431.5 3.7 copy-start.13
  431.5 4.8 %copy-start.14 = (bf16[2,352,2048]{2,1,0:T(8,128)(2,1)S(1)}, bf16[2,352,2048]{2,1,0:T(8,128)(2,1)}, u32[]{:S(2)}) copy-start(bf16[2,352,2048]{2,1,0:T(8,128)(2,1)} %get-tuple-element.102) | copy-start | bytes 8650756
  436.3 5.9 %copy-start.16 = (bf16[256,2048]{1,0:T(8,128)(2,1)S(1)}, bf16[256,2048]{1,0:T(8,128)(2,1)}, u32[]{:S(2)}) copy-start(bf16[256,2048]{1,0:T(8,128)(2,1)} %get-tuple-element.147) | copy-start | bytes 3145732

commit v2 on v1

--- a/solution.py
+++ b/solution.py
@@ -850,7 +850,7 @@
 class Weights:
     sends, locals, load = 0, 80, 0.0
 
-    def __init__(self, rows, grads, hidden, upstream, experts, units, common, own, at=0.0, pace=2.0):
+    def __init__(self, rows, grads, hidden, upstream, experts, units, common, own, at=0.0, pace=2.6):
         self.arrays = [rows, grads, hidden, upstream]
         self.in_spec = self.out_spec = ANY
         self.at, self.pace = at, pace
@@ -1163,7 +1163,7 @@
         def latent_back():
             grad, value = latent_sum[:, :rank].astype(jnp.float32), raw[...]
             inverse = lax.rsqrt(jnp.mean(value * value, axis=1, keepdims=True) + EPSILON)
-            gain_grad = jnp.sum(grad * value * inverse, axis=0, keepdims=True)
+            gain_part = jnp.sum(grad * value * inverse, axis=0, keepdims=True)
             scaled = grad * latent_gain[...]
             inner = jnp.mean(scaled * value, axis=1, keepdims=True)
             gl[:, :rank] = (inverse * scaled - value * (inverse * inverse * inverse * inner)).astype(low)
@@ -1171,26 +1171,30 @@
             sm[...] = small[...]
             part = rank // 8
             for j in range(8):
-                sm[j, 2:3, :part] = gain_grad[:, j * part : (j + 1) * part]
+                sm[j, 2:3, :part] = gain_part[:, j * part : (j + 1) * part]
             for n in range(0, gl.shape[1], 128):
                 turned[n : n + 128, :] = gl[:, n : n + 128].T
-
+            pre[...] = jnp.zeros_like(pre)
+
+        def latent_grad(quarter):
             def one(n, carry):
                 at = pl.ds(pl.multiple_of(n * tile, tile), tile)
                 lg[:, at] = matmul(turned[: lg.shape[0], :], normed[:, at]).astype(low)
                 return carry
 
-            lax.fori_loop(0, width // tile, one, 0)
-
-        def normed_back():
+            count = width // tile // 4
+            return lambda: lax.fori_loop(quarter * count, (quarter + 1) * count, one, 0)
+
+        def normed_grad(quarter):
             def one(n, carry):
                 at = pl.ds(pl.multiple_of(n * tile, tile), tile)
                 gn[:, at] = normed_sum[:, at].astype(jnp.float32) + matmul(gl[:, : latent.shape[0]], latent[:, at])
                 return carry
 
-            lax.fori_loop(0, width // tile, one, 0)
-            pre[...] = jnp.zeros_like(pre)
-
+            count = width // tile // 4
+            return lambda: lax.fori_loop(quarter * count, (quarter + 1) * count, one, 0)
+
+        def normed_back(quarter):
             def some(i, carry):
                 at = pl.ds(pl.multiple_of(i * 16, 16), 16)
                 value, grad = hidden[at].astype(jnp.float32), gn[at]
@@ -1202,15 +1206,21 @@
                 out[at] = (grad_middle[at] + back).astype(low)
                 return carry
 
-            lax.fori_loop(0, length // 16, some, 0)
+            count = length // 16 // 4
+            return lambda: lax.fori_loop(quarter * count, (quarter + 1) * count, some, 0)
+
+        def gain_grad():
             part = width // 8
             for j in range(8):
                 sm[j, 0:1, :] = pre[:, j * part : (j + 1) * part]
 
-        return [
-            (self.latent_line.finish() + 0.1, latent_back),
-            (self.normed_line.finish() + 0.1, normed_back),
-        ]
+        t = self.latent_line.finish() + 0.1
+        result = [(t, latent_back)] + [(t + 1.5 + 0.8 * i, latent_grad(i)) for i in range(4)]
+        t = self.normed_line.finish() + 0.1
+        result += [(t + 0.8 * i, normed_grad(i)) for i in range(4)]
+        result += [(t + 3.2 + 1.2 * i, normed_back(i)) for i in range(4)]
+        result.append((t + 8.0, gain_grad))
+        return result
 
 
 def lanes(width):
@@ -1546,7 +1556,7 @@
                 *swaps,
                 Line(mixture_own, at=0.1),
                 Scatter(shape((latent_full.shape[0], D), low), axis=1, pieces=2, at=24.0, source=tail.latent_source),
-                Scatter(shape(small_grad.shape, jnp.float32), at=52.0, source=tail.small_source),
+                Scatter(shape(small_grad.shape, jnp.float32), at=51.5, source=tail.small_source),
                 tail,
             ],
             5,

time: 451 us -> 448 us (level)
  no operation moved by 1% of the time
where the time goes in v2:
time: 448 us; the launch traced here: 440 us
  Pallas kernels  369 us (82%)
  other arithmetic  32.5 us (7%)
  local copies, waits for them, and re-layouts  20.6 us (5%)
  matrix products  16.4 us (4%)
    pallas_call x4, Pallas kernels, exchange(): pl.pallas_call(kernel, out_shape=[out for task in tasks for out in task.o...  264 us
    pallas_call x1, Pallas kernels, expert_stage(): pl.pallas_call(kernel, out_shape=[shape((4, pair, width), low), shape((4,...  105 us

profile of v2, /device:TPU:0, one launch (start us, length us, event | category | flops | bytes accessed | tf_op | source)
XLA Modules:
  0.0 440.0 jit_solution(6275296030802642951)
XLA Ops:
  1.8 0.7 broadcast_in_dim.12
  2.4 0.7 pad.16
  3.1 0.7 broadcast_in_dim.13
  3.8 0.7 fusion.23
  4.5 1.9 concatenate.23.refs_0_
  6.6 1.5 copy.86.refs_9_
  8.1 1.2 fusion.28
  9.3 0.7 copy.107
  10.0 0.7 copy.106
  10.7 48.5 %exchange_0.1 = (bf16[8,24,256]{2,1,0:T(8,128)(2,1)}, bf16[576,2048]{1,0:T(8,128)(2,1)}, bf16[8,256,768]{2,1,0:T(8,128)(2,1)}, bf16[8,64,1024]{2,1,0:T(8,128)(2,1)}, bf16[512,2048]{1,0:T(8,128)(2,1)}) custom-call(bf16[24,256]{1,0:T(8,128)(2,1)} %concatenate.23.refs_0_, bf16[576,256]{1,0:T(8,128)(2,1)} %bitcast.135, bf16[256,768]{1,0:T(8,128)(2,1)} %refs_2_.1, ...), custom_call_target="tpu_custom_call" | custom-call | tf_op jit(solution)/shard_map/exchange_0/pallas_call | solution.py:501
  59.2 0.7 convert_reduce_fusion
  59.9 0.7 reshape.256.refs_6_.refs_10_
  60.6 0.8 slice_convert_fusion
  61.4 0.9 slice_bitcast_fusion
  62.9 65.1 %exchange_1.1 = (bf16[8,256,2048]{2,1,0:T(8,128)(2,1)}, bf16[8,88,256]{2,1,0:T(8,128)(2,1)}, bf16[8,88,256]{2,1,0:T(8,128)(2,1)}, bf16[8,88,256]{2,1,0:T(8,128)(...) custom-call(bf16[256,2048]{1,0:T(8,128)(2,1)} %refs_0_.1, ...), custom_call_target="tpu_custom_call" | custom-call | tf_op jit(solution)/shard_map/exchange_1/pallas_call | solution.py:501
  128.1 1.9 copy.113
  129.9 2.1 multiply_reduce_fusion.2
  132.1 0.8 copy.102
  133.2 1.0 fusion.30
  134.7 1.0 copy-done.6
  136.3 0.7 fusion.24.mix_h
  137.0 105.1 %expert_stage.1 = (bf16[4,512,2048]{2,1,0:T(8,128)(2,1)}, bf16[4,512,2048]{2,1,0:T(8,128)(2,1)}, bf16[4,512,896]{2,1,0:T(8,128)(2,1)}, bf16[4,512,1792]{2,1,0:T(...) custom-call(bf16[256,2048]{1,0:T(8,128)(2,1)} %copy-done.6, bf16[256,128]{1,0:T(8,128)(2,1)} %fusion.24.mix_h, ...), custom_call_target="tpu_custom_call" | custom-call | tf_op jit(solution)/shard_map/expert_stage/pallas_call | solution.py:808
  242.1 63.9 %exchange_4.1 = (bf16[256,2048]{1,0:T(8,128)(2,1)}, bf16[256,128]{1,0:T(8,128)(2,1)}, bf16[256,2048]{1,0:T(8,128)(2,1)}, bf16[2,352,2048]{2,1,0:T(8,128)(2,1)}, ...) custom-call(bf16[256,2048]{1,0:T(8,128)(2,1)} %get-tuple-element.72., ...), custom_call_target="tpu_custom_call" | custom-call | tf_op jit(solution)/shard_map/exchange_4/pallas_call | solution.py:501
  306.0 1.1 fusion.17
  307.2 1.0 fusion.21
  308.1 1.5 fusion.32
  309.7 2.3 multiply_reduce_fusion
  312.0 1.0 subtract_add_fusion.refs_15_
  313.6 1.5 convolution_convert_fusion.5
  315.1 1.1 copy.124
  316.2 1.5 pad_maximum_fusion.1.refs_16_
  321.3 2.0 convolution_convert_fusion.2.refs_1_
  323.9 0.8 pad_maximum_fusion.refs_0_
  324.6 1.5 convolution_convert_fusion.3
  326.1 2.1 convolution_convert_fusion.1.refs_4_
  328.2 2.7 convolution_convert_fusion
  330.9 86.2 %exchange_5.1 = (bf16[256,640]{1,0:T(8,128)(2,1)}, bf16[256,2048]{1,0:T(8,128)(2,1)}, bf16[256,768]{1,0:T(8,128)(2,1)}, bf16[64,1024]{1,0:T(8,128)(2,1)}, bf16[5...) custom-call(bf16[256,640]{1,0:T(8,128)(2,1)} %pad_maximum_fusion.ref, ...), custom_call_target="tpu_custom_call" | custom-call | tf_op jit(solution)/shard_map/exchange_5/pallas_call | solution.py:501
  417.2 3.5 add_convert_fusion
  422.3 0.7 convert_element_type.252
  423.1 0.8 convert_element_type.253
  423.9 0.9 convert_bitcast_fusion.4
  424.8 0.9 bitcast_convert_fusion
  425.7 0.9 convert_element_type.249
  426.6 1.3 convert_bitcast_fusion.2
  427.9 3.7 convert_element_type.258
  431.6 1.1 copy-done.14
  432.7 5.9 %convert_bitcast_fusion = (f32[2,2048,352]{1,2,0:T(8,128)}, f32[2,2048,352]{1,2,0:T(8,128)}) fusion(bf16[2,352,2048]{2,1,0:T(8,128)(2,1)S(1)} %copy-done.14, bf16[2,352,2048]{2,1,0:T(8,128)(2,1)S(1)} %copy-done.13), kind=kLoop, calls=%fused_computation | loop fusion | flops 2883584 | bytes 17301504 | tf_op jit(solution)/shard_map/transpose | solution.py:1612
  438.6 1.0 copy.139
  (115 shorter events, 9.8 us)
Async XLA Ops:
  0.7 59.3 %copy-start.38 = (f32[32]{0:T(128)}, f32[32]{0:T(128)S(1)}, u32[]{:S(2)}) copy-start(f32[32]{0:T(128)S(1)} %multiply_exponential_fusion) | copy-start | bytes 388
  9.3 53.6 %copy-start.15 = (f32[256,32]{1,0:T(8,128)}, f32[256,32]{1,0:T(8,128)S(1)}, u32[]{:S(2)}) copy-start(f32[256,32]{1,0:T(8,128)S(1)} %get-tuple-element.120.refs_7_) | copy-start | bytes 98308
  62.3 72.4 %copy-start.34 = (bf16[8,2,8,256]{3,2,0,1:T(8,128)(2,1)}, bf16[8,2,8,256]{3,2,0,1:T(8,128)(2,1)S(1)}, u32[]{:S(2)}) copy-start(bf16[8,2,8,256]{3,2,0,1:T(8,128)(2,1)S(1)} %copy.126) | copy-start | bytes 196612
  128.0 4.0 copy-start.33
  128.1 4.8 %copy-start.20 = (bf16[256,1024]{1,0:T(8,128)(2,1)S(1)}, bf16[256,1024]{1,0:T(8,128)(2,1)}, u32[]{:S(2)}) copy-start(bf16[256,1024]{1,0:T(8,128)(2,1)} %get-tuple-element.80) | copy-start | bytes 1572868
  129.9 4.2 copy-start
  129.9 4.2 copy-start.3
  134.7 1.0 copy-start.6
  242.1 67.5 %copy-start.35 = (bf16[8,2,8,256]{3,2,0,1:T(8,128)(2,1)S(1)}, bf16[8,2,8,256]{3,2,0,1:T(8,128)(2,1)}, u32[]{:S(2)}) copy-start(bf16[8,2,8,256]{3,2,0,1:T(8,128)(2,1)} %copy-done.34) | copy-start | bytes 196612
  306.0 3.6 copy-start.1
  306.0 3.6 copy-start.4
  309.7 2.3 copy-start.9
  312.0 1.6 copy-start.8
  313.6 12.5 %copy-start.2 = (f32[256,2048]{1,0:T(8,128)}, f32[256,2048]{1,0:T(8,128)S(1)}, u32[]{:S(2)}) copy-start(f32[256,2048]{1,0:T(8,128)S(1)} %subtract_add_fusion.refs_15_) | copy-start | bytes 6291460
  313.6 2.6 copy-start.40
  313.6 4.1 copy-start.5
  316.2 1.8 copy-start.17
  318.0 1.0 copy-start.19
  318.5 0.9 copy-start.21
  318.5 1.3 copy-start.39
  318.5 2.0 copy-start.18
  318.9 1.8 copy-start.36
  319.0 2.0 copy-start.30
  319.0 2.0 copy-start.31
  319.4 1.9 copy-start.11
  321.3 2.0 copy-start.10
  323.3 1.3 copy-start.28
  323.4 2.7 copy-start.27
  326.1 2.1 copy-start.7
  417.1 3.5 copy-start.37
  417.1 5.2 %copy-start.32 = (bf16[64,1024]{1,0:T(8,128)(2,1)S(1)}, bf16[64,1024]{1,0:T(8,128)(2,1)}, u32[]{:S(2)}) copy-start(bf16[64,1024]{1,0:T(8,128)(2,1)} %get-tuple-element.95) | copy-start | bytes 393220
  417.1 5.9 %copy-start.29 = (bf16[512,256]{1,0:T(8,128)(2,1)S(1)}, bf16[512,256]{1,0:T(8,128)(2,1)}, u32[]{:S(2)}) copy-start(bf16[512,256]{1,0:T(8,128)(2,1)} %get-tuple-element.96) | copy-start | bytes 786436
  417.1 6.7 %copy-start.26 = (bf16[576,256]{1,0:T(8,128)(2,1)S(1)}, bf16[576,256]{1,0:T(8,128)(2,1)}, u32[]{:S(2)}) copy-start(bf16[576,256]{1,0:T(8,128)(2,1)} %get-tuple-element.94) | copy-start | bytes 884740
  420.6 4.1 copy-start.23
  420.6 5.0 %copy-start.22 = (bf16[256,768]{1,0:T(8,128)(2,1)S(1)}, bf16[256,768]{1,0:T(8,128)(2,1)}, u32[]{:S(2)}) copy-start(bf16[256,768]{1,0:T(8,128)(2,1)} %get-tuple-element.93) | copy-start | bytes 1179652
  422.3 4.3 copy-start.24
  422.3 4.3 copy-start.25
  424.7 3.1 copy-start.12
  427.9 3.7 copy-start.13
  427.9 4.8 %copy-start.14 = (bf16[2,352,2048]{2,1,0:T(8,128)(2,1)S(1)}, bf16[2,352,2048]{2,1,0:T(8,128)(2,1)}, u32[]{:S(2)}) copy-start(bf16[2,352,2048]{2,1,0:T(8,128)(2,1)} %get-tuple-element.102) | copy-start | bytes 8650756
  432.6 5.9 %copy-start.16 = (bf16[256,2048]{1,0:T(8,128)(2,1)S(1)}, bf16[256,2048]{1,0:T(8,128)(2,1)}, u32[]{:S(2)}) copy-start(bf16[256,2048]{1,0:T(8,128)(2,1)} %get-tuple-element.147) | copy-start | bytes 3145732
